TPU v7x, 256 devices: a whole 4x4x8 slice. The times are simulated.
256 devices in a mesh: unit: 4 (over y), bank: 4 (over x), zero: 16 (over z, core).
Axes of the slice: x: 4, y: 4, z: 8, core: 2. Of those that a mesh axis runs over, the one named last changes fastest.
Arguments:
- train_down: float32 [256, 1024, 2048], P(('unit', 'bank'), None, 'zero'), parts along dimension 0, may hold values from -0.25 to 0.25
- router_weight: float32 [8192, 64], P(('unit', 'zero'), 'bank'), parts along dimension 0, may hold values from -0.125 to 0.125
- router_gain: float32 [8192], P(('unit', 'zero')), parts along dimension 0, may hold values from 0.25 to 1.75
Outputs:
- ready_down: bfloat16 [256, 1024, 2048], P(('unit', 'bank'), 'zero'), parts along dimension 0
- scale_down: float32 [256, 1024], P(('unit', 'bank'), 'zero'), parts along dimension 0
- serve_router: bfloat16 [8192, 64], P('unit'), parts along dimension 0
There are 4 independent parts, one for each index of `unit`. A program takes and returns all parts, laid end to end along the dimension named above; each array names one. Nothing has to cross between parts.
All inputs are finite; a program needn't handle non-finite values.
Results may differ from a plain program's by a relative error of at most 0.001.
Values may be sent and summed in bfloat16 or wider, within the bound.
No kernel may reach another device: no remote copies, remote signals or barrier semaphores. Data moves between devices by JAX's collectives and lax.ppermute only.
A program may use at most 128 MiB of HBM per device.

v0:
```python
import functools

import jax
import jax.numpy as jnp
from jax import lax
from jax.experimental import pallas as pl
from jax.experimental.pallas import tpu as pltpu
from jax.sharding import Mesh
from jax.sharding import PartitionSpec as P


ZERO = ("zero_0", "zero_1")
UNIT_ZERO = ("unit", "zero_0", "zero_1")

RAW = (((4, 0), 0, 7), ((2, 0), 0, 6), ((-2, 0), 0, 5), ((2, 1), 0, 6), ((-2, 1), 0, 8))
FIRST = (0,)
PIECES = (
    ((3, 0), 0, 16),
    ((-3, 0), 0, 16),
    ((4, 0), 7, 9),
    ((1, 0), 0, 16),
    ((-1, 0), 0, 16),
    ((3, 1), 0, 16),
    ((-3, 1), 0, 16),
    ((4, 1), 0, 16),
    ((0, 1), 0, 16),
    ((1, 1), 0, 16),
    ((-1, 1), 0, 16),
    ((2, 0), 6, 10),
    ((-2, 0), 5, 11),
    ((2, 1), 6, 10),
    ((-2, 1), 8, 8),
)
GROUPS = (10, 6, 3, 2)
VMEM = pl.BlockSpec(memory_space=pltpu.VMEM)
ANY = pl.BlockSpec(memory_space=pl.ANY)
LIMIT = 4 * 1024 * 1024
WIDE = 50 * 1024 * 1024


def maxima_kernel(pieces, x_ref, out_ref, *refs):
    held_ref, sems, pick_sems = refs[len(pieces) :]
    experts, owners = x_ref.shape[0], out_ref.shape[0]
    lane = lax.broadcasted_iota(jnp.int32, (8, 128), 1)

    def copy(e):
        return pltpu.make_async_copy(x_ref.at[e], held_ref.at[e], sems.at[e])

    for e in range(experts):
        copy(e).start()
    picks = [pick(piece, x_ref, ref, pick_sems.at[i]) for i, (piece, ref) in enumerate(zip(pieces, refs))]
    for each in picks:
        each.start()

    @pl.loop(0, experts // 4)
    def _(g):
        for e in range(4):
            copy(g * 4 + e).wait()
        for k in range(owners):
            tile = jnp.where(g == 0, jnp.zeros((8, 128), jnp.float32), out_ref[k])
            for e in range(4):
                for r in range(8):
                    row = k * 64 + r * 8
                    top = jnp.max(jnp.abs(held_ref[g * 4 + e, row : row + 8, :]), axis=1, keepdims=True)
                    tile = jnp.where(lane == (g * 4 + e) * 8 + r, top, tile)
            out_ref[k] = tile

    for each in picks:
        each.wait()


def local_maxima(x, pieces):
    experts, rows, lanes = x.shape
    picks = [jax.ShapeDtypeStruct((piece[2], 64, lanes), jnp.float32) for piece in pieces]
    return pl.pallas_call(
        functools.partial(maxima_kernel, pieces),
        in_specs=[ANY],
        out_specs=[VMEM] * (1 + len(picks)),
        out_shape=[jax.ShapeDtypeStruct((rows // 64, 8, 128), jnp.float32)] + picks,
        scratch_shapes=[
            pltpu.VMEM(x.shape, jnp.float32),
            pltpu.SemaphoreType.DMA((experts,)),
            pltpu.SemaphoreType.DMA((len(picks),)),
        ],
        compiler_params=pltpu.CompilerParams(vmem_limit_bytes=WIDE),
        name="local_maxima",
    )(x)


def combine_kernel(got_ref, weight_ref, gain_ref, own_ref, out_ref):
    own = jnp.max(got_ref[...], axis=0)
    own_ref[...] = own
    router = weight_ref[...] * gain_ref[...]
    for k in range(out_ref.shape[0]):
        out_ref[k, 0:8, :] = own
        out_ref[k, 8:24, :] = router


def combined(got, weight, gain):
    return pl.pallas_call(
        combine_kernel,
        in_specs=[VMEM] * 3,
        out_specs=[VMEM] * 2,
        out_shape=[
            jax.ShapeDtypeStruct((8, 128), jnp.float32),
            jax.ShapeDtypeStruct((got.shape[0], 24, 128), jnp.float32),
        ],
        compiler_params=pltpu.CompilerParams(vmem_limit_bytes=LIMIT),
        name="combine",
    )(got, weight, gain)


def device_at(offset):
    z, c = lax.axis_index("zero_0"), lax.axis_index("zero_1")
    return lax.rem(z + offset[0] + 8, 8) * 2 + lax.rem(c + offset[1], 2)


def pick(piece, x_ref, out_ref, sem):
    offset, start, count = piece
    first = pl.multiple_of(device_at(offset) * 64, 64)
    return pltpu.make_async_copy(x_ref.at[pl.ds(start, count), pl.ds(first, 64), :], out_ref, sem)


def pick_kernel(piece, x_ref, out_ref, sem):
    copy = pick(piece, x_ref, out_ref, sem)
    copy.start()
    copy.wait()


def picked(piece, x):
    return pl.pallas_call(
        functools.partial(pick_kernel, piece),
        in_specs=[ANY],
        out_specs=VMEM,
        out_shape=jax.ShapeDtypeStruct((piece[2], 64, 128), jnp.float32),
        scratch_shapes=[pltpu.SemaphoreType.DMA],
        compiler_params=pltpu.CompilerParams(vmem_limit_bytes=WIDE),
        cost_estimate=pl.CostEstimate(flops=2000000, bytes_accessed=piece[2] * 64 * 128 * 8, transcendentals=0),
        name="pick",
    )(x)


def divide_rows(rows_ref, out_ref, scale, experts, start):
    for e in experts:
        for r in range(0, 8, 2):
            lane = (start + e) * 8 + r
            both = jnp.concatenate([scale[:, lane : lane + 1], scale[:, lane + 1 : lane + 2]], axis=0)
            out_ref[e, r * 8 : r * 8 + 16, :] = (rows_ref[e, r * 8 : r * 8 + 16, :] / both).astype(jnp.bfloat16)


def divide_kernel(piece, x_ref, scales_ref, out_ref, rows_ref, sems):
    offset, start, count = piece
    k = device_at(offset)
    first = pl.multiple_of(k * 64, 64)
    parts = [range(e, min(e + 4, count)) for e in range(0, count, 4)]
    copies = [
        pltpu.make_async_copy(
            x_ref.at[pl.ds(start + part[0], len(part)), pl.ds(first, 64), :],
            rows_ref.at[pl.ds(part[0], len(part))],
            sems.at[i],
        )
        for i, part in enumerate(parts)
    ]
    for copy in copies:
        copy.start()
    scale = scales_ref[k, 0:8, :]
    for copy, part in zip(copies, parts):
        copy.wait()
        divide_rows(rows_ref, out_ref, scale, part, start)


def divided(piece, x, scales):
    count = piece[2]
    return pl.pallas_call(
        functools.partial(divide_kernel, piece),
        in_specs=[ANY, VMEM],
        out_specs=VMEM,
        out_shape=jax.ShapeDtypeStruct((count, 64, 128), jnp.bfloat16),
        scratch_shapes=[pltpu.VMEM((count, 64, 128), jnp.float32), pltpu.SemaphoreType.DMA((pl.cdiv(count, 4),))],
        compiler_params=pltpu.CompilerParams(vmem_limit_bytes=WIDE),
        cost_estimate=pl.CostEstimate(flops=count * 64 * 128 * 8, bytes_accessed=count * 64 * 128 * 6, transcendentals=0),
        name="divide",
    )(x, scales)


def finish_kernel(piece, rows_ref, own_ref, out_ref):
    divide_rows(rows_ref, out_ref, own_ref[...], range(piece[2]), piece[1])


def finished(piece, rows, own):
    count = piece[2]
    return pl.pallas_call(
        functools.partial(finish_kernel, piece),
        in_specs=[VMEM, VMEM],
        out_specs=VMEM,
        out_shape=jax.ShapeDtypeStruct((count, 64, 128), jnp.bfloat16),
        compiler_params=pltpu.CompilerParams(vmem_limit_bytes=LIMIT),
        cost_estimate=pl.CostEstimate(flops=count * 64 * 128 * 8, bytes_accessed=count * 64 * 128 * 6, transcendentals=0),
        name="finish",
    )(rows, own)


def place_kernel(pieces, held, routed, *refs):
    n = len(pieces)
    blocks, refs = refs[:n], refs[n + held :]
    out_ref, sems = refs[routed], refs[-1]
    copies = []
    for i, (offset, start, count) in enumerate(pieces):
        column = pl.multiple_of(device_at((-offset[0], offset[1])) * 128, 128)
        target = out_ref.at[pl.ds(start, count), :, pl.ds(column, 128)]
        copies.append(pltpu.make_async_copy(blocks[i], target, sems.at[i]))
    if routed:
        copies.append(pltpu.make_async_copy(refs[0], refs[2], sems.at[n]))
    for copy in copies:
        copy.start()
    for copy in copies:
        copy.wait()


def placed(pieces, blocks, shape, into=None, router=None):
    n, held, routed = len(pieces), int(into is not None), int(router is not None)
    size = sum(piece[2] for piece in pieces) * 64 * 128
    shapes = [jax.ShapeDtypeStruct(shape, jnp.bfloat16)]
    if routed:
        shapes.append(jax.ShapeDtypeStruct(router.shape, router.dtype))
    return pl.pallas_call(
        functools.partial(place_kernel, tuple(pieces), held, routed),
        in_specs=[VMEM] * n + [ANY] * held + [VMEM] * routed,
        out_specs=[ANY] * (1 + routed),
        out_shape=shapes,
        scratch_shapes=[pltpu.SemaphoreType.DMA((n + routed,))],
        input_output_aliases={n: 0} if held else {},
        compiler_params=pltpu.CompilerParams(vmem_limit_bytes=LIMIT),
        cost_estimate=pl.CostEstimate(flops=size, bytes_accessed=size * 4, transcendentals=0),
        name="place",
    )(*blocks, *([into] if held else []), *([router] if routed else []))


def sent(piece, offset):
    pairs = [(z * 2 + c, ((z + offset[0]) % 8) * 2 + (c + offset[1]) % 2) for z in range(8) for c in range(2)]
    return lax.ppermute(piece, ZERO, pairs)


def exchanged(value):
    return lax.all_to_all(value, ZERO, 0, 0, tiled=True)


def sent_raw(i, rows):
    return sent(rows, RAW[i][0])


def per_device(train_down, router_weight, router_gain):
    experts = train_down.shape[0]
    rows = [picked(RAW[i], train_down) for i in FIRST]
    maxima, *more = local_maxima(train_down, RAW[len(FIRST) :])
    raw = [sent_raw(i, r) for i, r in enumerate(rows + more)]
    got = exchanged(maxima)
    own, payload = combined(got, router_weight.T, router_gain[None, :])
    shared = exchanged(payload)

    kept = ((0, 0), 0, experts)
    blocks = []
    for piece in PIECES:
        blocks.append(sent(divided(piece, train_down, shared), piece[0]))

    rows = shared[:, 8:24, :].astype(jnp.bfloat16).transpose(1, 0, 2).reshape(16, 2048)
    rows, _ = lax.optimization_barrier((rows, blocks[2]))
    router = lax.all_gather(rows, "bank", axis=0, tiled=True)

    early = [divided(kept, train_down, shared)] + [finished(p, r, own) for p, r in zip(RAW, raw)]
    pieces, blocks = (kept,) + RAW + PIECES, early + blocks
    shape = (experts, 64, 2048)
    ready_down, first = None, 0
    for i, n in enumerate(GROUPS):
        group = slice(first, first + n)
        out = placed(pieces[group], blocks[group], shape, ready_down, router if i == 1 else None)
        ready_down, first = out[0], first + n
        if i == 1:
            serve_router = out[1].T

    scale_down = own.reshape(8, 16, 8).transpose(1, 2, 0).reshape(16, 64)
    return (ready_down, scale_down, serve_router)


def solution(mesh):
    torus = Mesh(
        mesh.devices.reshape(mesh.shape["unit"], mesh.shape["bank"], 8, 2),
        ("unit", "bank", "zero_0", "zero_1"),
    )
    placed_at = (P(("unit", "bank"), None, ZERO), P(UNIT_ZERO, "bank"), P(UNIT_ZERO))
    return jax.shard_map(
        per_device,
        mesh=torus,
        in_specs=placed_at,
        out_specs=(P(("unit", "bank"), ZERO, None), P(("unit", "bank"), ZERO), P("unit", None)),
        check_vma=False,
    )
```

profile of v0, /device:TPU:2, one launch (start us, length us, event | category | flops | bytes accessed | tf_op | source)
XLA Modules:
  0.0 156.5 jit_solution(9691334308850530562)
XLA Ops:
  0.7 5.0 %local_maxima.1 = (f32[16,8,128]{2,1,0:T(8,128)S(1)}, f32[6,64,128]{2,1,0:T(8,128)S(1)}, f32[5,64,128]{2,1,0:T(8,128)S(1)}, f32[6,64,128]{2,1,0:T(8,128)S(1)}, f32[8,64,128]{2,1,0:T(8,128)}) custom-call(f32[16,1024,128]{2,1,0:T(8,128)} %x_ref.35), custom_call_target="tpu_custom_call" | custom-call | tf_op jit(solution)/shard_map/local_maxima/pallas_call | solution.py:75
  5.7 16.2 %all_to_all.10.got_ref = f32[16,8,128]{2,1,0:T(8,128)S(1)} all-to-all(f32[16,8,128]{2,1,0:T(8,128)S(1)} %get-tuple-element.13), channel_id=1, replica_groups=mesh['unit'=4,'bank'=4,'zero_0'=8,'zero_1'=2] {'zero_0','zero_1'}, dimensions={0} | all-to-all | bytes 131072 | tf_op jit(solution)/shard_map/all_to_all | solution.py:245
  22.6 3.5 %all-to-all-start.1 = ((f32[16,24,128]{2,1,0:T(8,128)}), f32[16,24,128]{2,1,0:T(8,128)S(1)}, u32[]{:S(2)}, u32[]{:S(2)}) async-start(f32[16,24,128]{2,1,0:T(8,128)} %get-tuple-element.14), calls=%async_computation.1 | async-start | bytes 393216 | tf_op jit(solution)/shard_map/all_to_all | solution.py:245
  27.1 5.8 %collective-permute-start.11 = (f32[7,64,128]{2,1,0:T(8,128)S(1)}, f32[7,64,128]{2,1,0:T(8,128)S(1)}, u32[]{:S(2)}, u32[]{:S(2)}) collective-permute-start(f32[7,64,128]{2,1,0:T(8,128)S(1)} %pick.1), channel_id=1, source_target_pairs={{0,8},{1,9},{2,10},{3,11},{4,12},{5,13},{6,14},{7,15},{8,0},{9,1},... | collective-permute-start | bytes 688136 | tf_op jit(solution)/shard_map/ppermute | solution.py:241
  33.5 3.5 %collective-permute-start.13 = (f32[5,64,128]{2,1,0:T(8,128)S(1)}, f32[5,64,128]{2,1,0:T(8,128)S(1)}, u32[]{:S(2)}, u32[]{:S(2)}) collective-permute-start(f32[5,64,128]{2,1,0:T(8,128)S(1)} %get-tuple-element.17), channel_id=1, source_target_pairs={{0,12},{1,13},{2,14},{3,15},{4,0},{5,1},{6,2},{7,3},{8,4},{9,5},{1... | collective-permute-start | bytes 491528 | tf_op jit(solution)/shard_map/ppermute | solution.py:241
  37.0 2.4 %collective-permute-start.15 = (f32[8,64,128]{2,1,0:T(8,128)}, f32[8,64,128]{2,1,0:T(8,128)S(1)}, u32[]{:S(2)}, u32[]{:S(2)}) collective-permute-start(f32[8,64,128]{2,1,0:T(8,128)} %get-tuple-element.19), channel_id=1, source_target_pairs={{0,13},{1,12},{2,15},{3,14},{4,1},{5,0},{6,3},{7,2},{8,5},{9,4},{1... | collective-permute-start | bytes 786440 | tf_op jit(solution)/shard_map/ppermute | solution.py:241
  39.4 1.5 divide.28
  40.9 1.5 divide.29
  42.4 1.5 divide.31
  43.9 1.5 divide.26
  45.4 12.7 %collective-permute-done.13.rows_ref = f32[5,64,128]{2,1,0:T(8,128)S(1)} collective-permute-done((f32[5,64,128]{2,1,0:T(8,128)S(1)}, f32[5,64,128]{2,1,0:T(8,128)S(1)}, u32[]{:S(2)}, u32[]{:S(2)}) %collective-permute-start.13) | collective-permute-done | bytes 163872 | tf_op jit(solution)/shard_map/ppermute | solution.py:241
  58.8 5.0 %collective-permute-start.17 = (bf16[16,64,128]{2,1,0:T(8,128)(2,1)S(1)}, bf16[16,64,128]{2,1,0:T(8,128)(2,1)S(1)}, u32[]{:S(2)}, u32[]{:S(2)}) collective-permute-start(bf16[16,64,128]{2,1,0:T(8,128)(2,1)S(1)} %divide.29), channel_id=1, source_target_pairs={{0,10},{1,11},{2,12},{3,13},{4,14},{5,15},{6,0},{7,1},{8,2},{9,3},... | collective-permute-start | bytes 786440 | tf_op jit(solution)/shard_map/ppermute | solution.py:241
  65.2 1.6 %collective-permute-start.10 = (bf16[16,64,128]{2,1,0:T(8,128)(2,1)S(1)}, bf16[16,64,128]{2,1,0:T(8,128)(2,1)S(1)}, u32[]{:S(2)}, u32[]{:S(2)}) collective-permute-start(bf16[16,64,128]{2,1,0:T(8,128)(2,1)S(1)} %divide.26), channel_id=1, source_target_pairs={{0,3},{1,2},{2,5},{3,4},{4,7},{5,6},{6,9},{7,8},{8,11},{9,10},{10,... | collective-permute-start | bytes 786440 | tf_op jit(solution)/shard_map/ppermute | solution.py:241
  68.1 2.8 %collective-permute-start.18 = (bf16[9,64,128]{2,1,0:T(8,128)(2,1)S(1)}, bf16[9,64,128]{2,1,0:T(8,128)(2,1)S(1)}, u32[]{:S(2)}, u32[]{:S(2)}) collective-permute-start(bf16[9,64,128]{2,1,0:T(8,128)(2,1)S(1)} %divide.30), channel_id=1, source_target_pairs={{0,8},{1,9},{2,10},{3,11},{4,12},{5,13},{6,14},{7,15},{8,0},{9,1},... | collective-permute-start | bytes 442376 | tf_op jit(solution)/shard_map/ppermute | solution.py:241
  71.0 2.2 %divide.21 = bf16[16,64,128]{2,1,0:T(8,128)(2,1)} custom-call(f32[16,1024,128]{2,1,0:T(8,128)} %x_ref.35, f32[16,24,128]{2,1,0:T(8,128)S(1)} %all-to-all-done.1.scales_ref), custom_call_target="tpu_custom_call" | custom-call | flops 1048576 | bytes 786432 | tf_op jit(solution)/shard_map/divide/pallas_call | solution.py:174
  73.2 2.2 %divide.22 = bf16[16,64,128]{2,1,0:T(8,128)(2,1)} custom-call(f32[16,1024,128]{2,1,0:T(8,128)} %x_ref.35, f32[16,24,128]{2,1,0:T(8,128)S(1)} %all-to-all-done.1.scales_ref), custom_call_target="tpu_custom_call" | custom-call | flops 1048576 | bytes 786432 | tf_op jit(solution)/shard_map/divide/pallas_call | solution.py:174
  75.4 1.5 divide.23
  76.9 1.5 divide.24
  78.4 1.5 divide.25
  79.9 17.7 %collective-permute-done.18.refs_8_ = bf16[9,64,128]{2,1,0:T(8,128)(2,1)S(1)} collective-permute-done((bf16[9,64,128]{2,1,0:T(8,128)(2,1)S(1)}, bf16[9,64,128]{2,1,0:T(8,128)(2,1)S(1)}, u32[]{:S(2)}, u32[]{:S(2)}) %collective-permute-start.18) | collective-permute-done | bytes 147488 | tf_op jit(solution)/shard_map/ppermute | solution.py:241
  98.3 3.5 %collective-permute-start.6 = (bf16[16,64,128]{2,1,0:T(8,128)(2,1)}, bf16[16,64,128]{2,1,0:T(8,128)(2,1)S(1)}, u32[]{:S(2)}, u32[]{:S(2)}) collective-permute-start(bf16[16,64,128]{2,1,0:T(8,128)(2,1)} %divide.22), channel_id=1, source_target_pairs={{0,7},{1,6},{2,9},{3,8},{4,11},{5,10},{6,13},{7,12},{8,15},{9,14},... | collective-permute-start | bytes 786440 | tf_op jit(solution)/shard_map/ppermute | solution.py:241
  103.1 3.2 %collective-permute-start.8 = (bf16[16,64,128]{2,1,0:T(8,128)(2,1)S(1)}, bf16[16,64,128]{2,1,0:T(8,128)(2,1)S(1)}, u32[]{:S(2)}, u32[]{:S(2)}) collective-permute-start(bf16[16,64,128]{2,1,0:T(8,128)(2,1)S(1)} %divide.24), channel_id=1, source_target_pairs={{0,9},{1,8},{2,11},{3,10},{4,13},{5,12},{6,15},{7,14},{8,1},{9,0},... | collective-permute-start | bytes 786440 | tf_op jit(solution)/shard_map/ppermute | solution.py:241
  107.4 1.5 copy.12
  109.0 1.4 copy.13
  120.4 1.5 divide.18
  121.9 1.7 %collective-permute-start.2 = (bf16[16,64,128]{2,1,0:T(8,128)(2,1)S(1)}, bf16[16,64,128]{2,1,0:T(8,128)(2,1)S(1)}, u32[]{:S(2)}, u32[]{:S(2)}) collective-permute-start(bf16[16,64,128]{2,1,0:T(8,128)(2,1)S(1)} %divide.18), channel_id=1, source_target_pairs={{0,15},{1,14},{2,1},{3,0},{4,3},{5,2},{6,5},{7,4},{8,7},{9,6},{10,... | collective-permute-start | bytes 786440 | tf_op jit(solution)/shard_map/ppermute | solution.py:241
  125.1 1.5 collective-permute-start.3
  126.6 3.8 %collective-permute-done.8.refs_3_ = bf16[16,64,128]{2,1,0:T(8,128)(2,1)S(1)} collective-permute-done((bf16[16,64,128]{2,1,0:T(8,128)(2,1)S(1)}, bf16[16,64,128]{2,1,0:T(8,128)(2,1)S(1)}, u32[]{:S(2)}, u32[]{:S(2)}) %collective-permute-start.8) | collective-permute-done | bytes 262176 | tf_op jit(solution)/shard_map/ppermute | solution.py:241
  130.4 4.4 %collective-permute-start = (bf16[10,64,128]{2,1,0:T(8,128)(2,1)S(1)}, bf16[10,64,128]{2,1,0:T(8,128)(2,1)S(1)}, u32[]{:S(2)}, u32[]{:S(2)}) collective-permute-start(bf16[10,64,128]{2,1,0:T(8,128)(2,1)S(1)} %divide.16), channel_id=1, source_target_pairs={{0,5},{1,4},{2,7},{3,6},{4,9},{5,8},{6,11},{7,10},{8,13},{9,12},{1... | collective-permute-start | bytes 491528 | tf_op jit(solution)/shard_map/ppermute | solution.py:241
  136.1 1.5 divide.27.refs_0_
  137.7 12.3 %all_gather.3.refs_7_ = bf16[64,2048]{1,0:T(8,128)(2,1)S(1)} all-gather(bf16[16,2048]{1,0:T(8,128)(2,1)S(1)} %copy_bitcast_fusion), channel_id=1, replica_groups=mesh['unit'=4,'bank'=4,'zero_0'=8,'zero_1'=2] {'bank'}, dimensions={0}, use_global_device_ids=true | all-gather | bytes 327680 | tf_op jit(solution)/shard_map/all_gather | solution.py:268
  153.7 1.9 %collective-permute-done.1.refs_1_ = bf16[8,64,128]{2,1,0:T(8,128)(2,1)S(1)} collective-permute-done((bf16[8,64,128]{2,1,0:T(8,128)(2,1)S(1)}, bf16[8,64,128]{2,1,0:T(8,128)(2,1)S(1)}, u32[]{:S(2)}, u32[]{:S(2)}) %collective-permute-start.1) | collective-permute-done | bytes 131104 | tf_op jit(solution)/shard_map/ppermute | solution.py:241
  (68 shorter events, 25.8 us)
Async XLA Ops:
  0.6 21.2 %copy-start.10 = (f32[128,16]{0,1:T(8,128)S(1)}, f32[128,16]{0,1:T(8,128)}, u32[]{:S(2)}) copy-start(f32[128,16]{0,1:T(8,128)} %param.4) | copy-start | bytes 24580
  0.6 21.2 %copy-start.11 = (f32[128]{0:T(128)S(1)}, f32[128]{0:T(128)}, u32[]{:S(2)}) copy-start(f32[128]{0:T(128)} %param.5) | copy-start | bytes 1540
  22.6 16.8 %all-to-all-start.1 = ((f32[16,24,128]{2,1,0:T(8,128)}), f32[16,24,128]{2,1,0:T(8,128)S(1)}, u32[]{:S(2)}, u32[]{:S(2)}) async-start(f32[16,24,128]{2,1,0:T(8,128)} %get-tuple-element.14), calls=%async_computation.1 | async-start | bytes 393216 | tf_op jit(solution)/shard_map/all_to_all | solution.py:245
  27.1 37.5 %collective-permute-start.11 = (f32[7,64,128]{2,1,0:T(8,128)S(1)}, f32[7,64,128]{2,1,0:T(8,128)S(1)}, u32[]{:S(2)}, u32[]{:S(2)}) collective-permute-start(f32[7,64,128]{2,1,0:T(8,128)S(1)} %pick.1), channel_id=1, source_target_pairs={{0,8},{1,9},{2,10},{3,11},{4,12},{5,13},{6,14},{7,15},{8,0},{9,1},... | collective-permute-start | bytes 688136 | tf_op jit(solution)/shard_map/ppermute | solution.py:241
  32.9 25.9 %collective-permute-start.12 = (f32[6,64,128]{2,1,0:T(8,128)S(1)}, f32[6,64,128]{2,1,0:T(8,128)S(1)}, u32[]{:S(2)}, u32[]{:S(2)}) collective-permute-start(f32[6,64,128]{2,1,0:T(8,128)S(1)} %get-tuple-element.16), channel_id=1, source_target_pairs={{0,4},{1,5},{2,6},{3,7},{4,8},{5,9},{6,10},{7,11},{8,12},{9,13},{1... | collective-permute-start | bytes 589832 | tf_op jit(solution)/shard_map/ppermute | solution.py:241
  33.5 30.3 %collective-permute-start.14 = (f32[6,64,128]{2,1,0:T(8,128)S(1)}, f32[6,64,128]{2,1,0:T(8,128)S(1)}, u32[]{:S(2)}, u32[]{:S(2)}) collective-permute-start(f32[6,64,128]{2,1,0:T(8,128)S(1)} %get-tuple-element.18), channel_id=1, source_target_pairs={{0,5},{1,4},{2,7},{3,6},{4,9},{5,8},{6,11},{7,10},{8,13},{9,12},{1... | collective-permute-start | bytes 589832 | tf_op jit(solution)/shard_map/ppermute | solution.py:241
  33.5 24.6 %collective-permute-start.13 = (f32[5,64,128]{2,1,0:T(8,128)S(1)}, f32[5,64,128]{2,1,0:T(8,128)S(1)}, u32[]{:S(2)}, u32[]{:S(2)}) collective-permute-start(f32[5,64,128]{2,1,0:T(8,128)S(1)} %get-tuple-element.17), channel_id=1, source_target_pairs={{0,12},{1,13},{2,14},{3,15},{4,0},{5,1},{6,2},{7,3},{8,4},{9,5},{1... | collective-permute-start | bytes 491528 | tf_op jit(solution)/shard_map/ppermute | solution.py:241
  37.0 31.1 %collective-permute-start.15 = (f32[8,64,128]{2,1,0:T(8,128)}, f32[8,64,128]{2,1,0:T(8,128)S(1)}, u32[]{:S(2)}, u32[]{:S(2)}) collective-permute-start(f32[8,64,128]{2,1,0:T(8,128)} %get-tuple-element.19), channel_id=1, source_target_pairs={{0,13},{1,12},{2,15},{3,14},{4,1},{5,0},{6,3},{7,2},{8,5},{9,4},{1... | collective-permute-start | bytes 786440 | tf_op jit(solution)/shard_map/ppermute | solution.py:241
  58.1 0.7 copy-start.6
  58.8 39.5 %collective-permute-start.16 = (bf16[16,64,128]{2,1,0:T(8,128)(2,1)S(1)}, bf16[16,64,128]{2,1,0:T(8,128)(2,1)S(1)}, u32[]{:S(2)}, u32[]{:S(2)}) collective-permute-start(bf16[16,64,128]{2,1,0:T(8,128)(2,1)S(1)} %divide.28), channel_id=1, source_target_pairs={{0,6},{1,7},{2,8},{3,9},{4,10},{5,11},{6,12},{7,13},{8,14},{9,15},... | collective-permute-start | bytes 786440 | tf_op jit(solution)/shard_map/ppermute | solution.py:241
  58.8 43.0 %collective-permute-start.17 = (bf16[16,64,128]{2,1,0:T(8,128)(2,1)S(1)}, bf16[16,64,128]{2,1,0:T(8,128)(2,1)S(1)}, u32[]{:S(2)}, u32[]{:S(2)}) collective-permute-start(bf16[16,64,128]{2,1,0:T(8,128)(2,1)S(1)} %divide.29), channel_id=1, source_target_pairs={{0,10},{1,11},{2,12},{3,13},{4,14},{5,15},{6,0},{7,1},{8,2},{9,3},... | collective-permute-start | bytes 786440 | tf_op jit(solution)/shard_map/ppermute | solution.py:241
  63.8 0.7 copy-start.4
  64.5 38.5 %collective-permute-start.19 = (bf16[16,64,128]{2,1,0:T(8,128)(2,1)S(1)}, bf16[16,64,128]{2,1,0:T(8,128)(2,1)S(1)}, u32[]{:S(2)}, u32[]{:S(2)}) collective-permute-start(bf16[16,64,128]{2,1,0:T(8,128)(2,1)S(1)} %divide.31), channel_id=1, source_target_pairs={{0,2},{1,3},{2,4},{3,5},{4,6},{5,7},{6,8},{7,9},{8,10},{9,11},{10,... | collective-permute-start | bytes 786440 | tf_op jit(solution)/shard_map/ppermute | solution.py:241
  64.5 0.7 copy-start.2
  65.2 41.0 %collective-permute-start.10 = (bf16[16,64,128]{2,1,0:T(8,128)(2,1)S(1)}, bf16[16,64,128]{2,1,0:T(8,128)(2,1)S(1)}, u32[]{:S(2)}, u32[]{:S(2)}) collective-permute-start(bf16[16,64,128]{2,1,0:T(8,128)(2,1)S(1)} %divide.26), channel_id=1, source_target_pairs={{0,3},{1,2},{2,5},{3,4},{4,7},{5,6},{6,9},{7,8},{8,11},{9,10},{10,... | collective-permute-start | bytes 786440 | tf_op jit(solution)/shard_map/ppermute | solution.py:241
  68.1 5.0 %copy-start = (f32[8,64,128]{2,1,0:T(8,128)}, f32[8,64,128]{2,1,0:T(8,128)S(1)}, u32[]{:S(2)}) copy-start(f32[8,64,128]{2,1,0:T(8,128)S(1)} %collective-permute-done.15.rows_ref) | copy-start | bytes 786436
  68.1 29.5 %collective-permute-start.18 = (bf16[9,64,128]{2,1,0:T(8,128)(2,1)S(1)}, bf16[9,64,128]{2,1,0:T(8,128)(2,1)S(1)}, u32[]{:S(2)}, u32[]{:S(2)}) collective-permute-start(bf16[9,64,128]{2,1,0:T(8,128)(2,1)S(1)} %divide.30), channel_id=1, source_target_pairs={{0,8},{1,9},{2,10},{3,11},{4,12},{5,13},{6,14},{7,15},{8,0},{9,1},... | collective-permute-start | bytes 442376 | tf_op jit(solution)/shard_map/ppermute | solution.py:241
  98.3 23.6 %collective-permute-start.5 = (bf16[16,64,128]{2,1,0:T(8,128)(2,1)}, bf16[16,64,128]{2,1,0:T(8,128)(2,1)S(1)}, u32[]{:S(2)}, u32[]{:S(2)}) collective-permute-start(bf16[16,64,128]{2,1,0:T(8,128)(2,1)} %divide.21), channel_id=1, source_target_pairs={{0,14},{1,15},{2,0},{3,1},{4,2},{5,3},{6,4},{7,5},{8,6},{9,7},{10,... | collective-permute-start | bytes 786440 | tf_op jit(solution)/shard_map/ppermute | solution.py:241
  98.3 25.4 %collective-permute-start.6 = (bf16[16,64,128]{2,1,0:T(8,128)(2,1)}, bf16[16,64,128]{2,1,0:T(8,128)(2,1)S(1)}, u32[]{:S(2)}, u32[]{:S(2)}) collective-permute-start(bf16[16,64,128]{2,1,0:T(8,128)(2,1)} %divide.22), channel_id=1, source_target_pairs={{0,7},{1,6},{2,9},{3,8},{4,11},{5,10},{6,13},{7,12},{8,15},{9,14},... | collective-permute-start | bytes 786440 | tf_op jit(solution)/shard_map/ppermute | solution.py:241
  101.8 23.3 %collective-permute-start.7 = (bf16[16,64,128]{2,1,0:T(8,128)(2,1)S(1)}, bf16[16,64,128]{2,1,0:T(8,128)(2,1)S(1)}, u32[]{:S(2)}, u32[]{:S(2)}) collective-permute-start(bf16[16,64,128]{2,1,0:T(8,128)(2,1)S(1)} %divide.23), channel_id=1, source_target_pairs={{0,11},{1,10},{2,13},{3,12},{4,15},{5,14},{6,1},{7,0},{8,3},{9,2},... | collective-permute-start | bytes 786440 | tf_op jit(solution)/shard_map/ppermute | solution.py:241
  103.1 27.4 %collective-permute-start.8 = (bf16[16,64,128]{2,1,0:T(8,128)(2,1)S(1)}, bf16[16,64,128]{2,1,0:T(8,128)(2,1)S(1)}, u32[]{:S(2)}, u32[]{:S(2)}) collective-permute-start(bf16[16,64,128]{2,1,0:T(8,128)(2,1)S(1)} %divide.24), channel_id=1, source_target_pairs={{0,9},{1,8},{2,11},{3,10},{4,13},{5,12},{6,15},{7,14},{8,1},{9,0},... | collective-permute-start | bytes 786440 | tf_op jit(solution)/shard_map/ppermute | solution.py:241
  106.3 28.6 %collective-permute-start.9 = (bf16[16,64,128]{2,1,0:T(8,128)(2,1)S(1)}, bf16[16,64,128]{2,1,0:T(8,128)(2,1)S(1)}, u32[]{:S(2)}, u32[]{:S(2)}) collective-permute-start(bf16[16,64,128]{2,1,0:T(8,128)(2,1)S(1)} %divide.25), channel_id=1, source_target_pairs={{0,1},{1,0},{2,3},{3,2},{4,5},{5,4},{6,7},{7,6},{8,9},{9,8},{10,11... | collective-permute-start | bytes 786440 | tf_op jit(solution)/shard_map/ppermute | solution.py:241
  110.4 0.9 copy-start.7
  111.7 0.9 copy-start.5
  112.8 0.9 copy-start.3
  113.9 1.0 copy-start.1
  121.9 30.9 %collective-permute-start.2 = (bf16[16,64,128]{2,1,0:T(8,128)(2,1)S(1)}, bf16[16,64,128]{2,1,0:T(8,128)(2,1)S(1)}, u32[]{:S(2)}, u32[]{:S(2)}) collective-permute-start(bf16[16,64,128]{2,1,0:T(8,128)(2,1)S(1)} %divide.18), channel_id=1, source_target_pairs={{0,15},{1,14},{2,1},{3,0},{4,3},{5,2},{6,5},{7,4},{8,7},{9,6},{10,... | collective-permute-start | bytes 786440 | tf_op jit(solution)/shard_map/ppermute | solution.py:241
  123.7 29.2 %collective-permute-start.4 = (bf16[11,64,128]{2,1,0:T(8,128)(2,1)S(1)}, bf16[11,64,128]{2,1,0:T(8,128)(2,1)S(1)}, u32[]{:S(2)}, u32[]{:S(2)}) collective-permute-start(bf16[11,64,128]{2,1,0:T(8,128)(2,1)S(1)} %divide.20), channel_id=1, source_target_pairs={{0,12},{1,13},{2,14},{3,15},{4,0},{5,1},{6,2},{7,3},{8,4},{9,5},{1... | collective-permute-start | bytes 540680 | tf_op jit(solution)/shard_map/ppermute | solution.py:241
  125.1 27.5 %collective-permute-start.3 = (bf16[10,64,128]{2,1,0:T(8,128)(2,1)S(1)}, bf16[10,64,128]{2,1,0:T(8,128)(2,1)S(1)}, u32[]{:S(2)}, u32[]{:S(2)}) collective-permute-start(bf16[10,64,128]{2,1,0:T(8,128)(2,1)S(1)} %divide.19), channel_id=1, source_target_pairs={{0,4},{1,5},{2,6},{3,7},{4,8},{5,9},{6,10},{7,11},{8,12},{9,13},{1... | collective-permute-start | bytes 491528 | tf_op jit(solution)/shard_map/ppermute | solution.py:241
  130.4 25.2 %collective-permute-start = (bf16[10,64,128]{2,1,0:T(8,128)(2,1)S(1)}, bf16[10,64,128]{2,1,0:T(8,128)(2,1)S(1)}, u32[]{:S(2)}, u32[]{:S(2)}) collective-permute-start(bf16[10,64,128]{2,1,0:T(8,128)(2,1)S(1)} %divide.16), channel_id=1, source_target_pairs={{0,5},{1,4},{2,7},{3,6},{4,9},{5,8},{6,11},{7,10},{8,13},{9,12},{1... | collective-permute-start | bytes 491528 | tf_op jit(solution)/shard_map/ppermute | solution.py:241
  134.8 20.8 %collective-permute-start.1 = (bf16[8,64,128]{2,1,0:T(8,128)(2,1)S(1)}, bf16[8,64,128]{2,1,0:T(8,128)(2,1)S(1)}, u32[]{:S(2)}, u32[]{:S(2)}) collective-permute-start(bf16[8,64,128]{2,1,0:T(8,128)(2,1)S(1)} %divide.17), channel_id=1, source_target_pairs={{0,13},{1,12},{2,15},{3,14},{4,1},{5,0},{6,3},{7,2},{8,5},{9,4},{1... | collective-permute-start | bytes 393224 | tf_op jit(solution)/shard_map/ppermute | solution.py:241
  136.1 13.9 %copy-start.9 = (bf16[9,64,128]{2,1,0:T(8,128)(2,1)S(1)}, bf16[9,64,128]{2,1,0:T(8,128)(2,1)}, u32[]{:S(2)}) copy-start(bf16[9,64,128]{2,1,0:T(8,128)(2,1)} %copy-done.8) | copy-start | bytes 442372
  (1 other events, 0.7 us)
where the time goes:
time: 159 us; the launch traced here: 157 us
  starting transfers between devices  44.1 us (28%)
  waiting for transfers between devices  36.5 us (23%)
  Pallas kernels  36.3 us (23%)
  blocking collectives  28.5 us (18%)
  local copies, waits for them, and re-layouts  10.1 us (6%)
    ppermute x20, starting transfers between devices, sent(): return lax.ppermute(piece, ZERO, pairs)  40.6 us
    ppermute x20, waiting for transfers between devices, sent(): return lax.ppermute(piece, ZERO, pairs)  36.5 us
    pallas_call x16, Pallas kernels, divided(): pl.pallas_call(functools.partial(divide_kernel, piece), in_specs=[ANY, VM...  24.5 us
    all_to_all x1, blocking collectives, exchanged(): return lax.all_to_all(value, ZERO, 0, 0, tiled=True)  16.2 us
    all_gather x1, blocking collectives, per_device(): router = lax.all_gather(rows, 'bank', axis=0, tiled=True)  12.3 us
    unnamed x25, local copies, waits for them, and re-layouts  7.86 us
    pallas_call x1, Pallas kernels, local_maxima(): pl.pallas_call(functools.partial(maxima_kernel, pieces), in_specs=[ANY],...  5.05 us
    pallas_call x4, Pallas kernels, placed(): pl.pallas_call(functools.partial(place_kernel, tuple(pieces), held, route...  4.13 us
  transfers between devices with their start and end apart: 21, of which 5 were waited for; matrix products, arithmetic and copies ran while one was open for 2% of the time, Pallas kernels for 19%

commit v1 on v0

v1 whole, which is shorter than its diff:
```python
import functools

import jax
import jax.numpy as jnp
from jax import lax
from jax.experimental import pallas as pl
from jax.experimental.pallas import tpu as pltpu
from jax.sharding import Mesh
from jax.sharding import PartitionSpec as P


ZERO = ("zero_0", "zero_1")
UNIT_ZERO = ("unit", "zero_0", "zero_1")

OWN, OTHER = -1, -2
RAW = (((4, 0), 0, 8), ((2, 0), 0, 5), ((-2, 0), 0, 7))
PIECES = (
    ((3, 0), OWN, 8),
    ((-3, 0), OWN, 8),
    ((4, 0), 8, 8),
    ((3, 1), 0, 16),
    ((-3, 1), 0, 16),
    ((1, 0), 0, 16),
    ((-1, 0), 0, 16),
    ((4, 1), 0, 16),
    ((3, 0), OTHER, 8),
    ((-3, 0), OTHER, 8),
    ((0, 1), 0, 16),
    ((1, 1), 0, 16),
    ((-1, 1), 0, 16),
    ((2, 0), 5, 11),
    ((-2, 0), 7, 9),
    ((2, 1), 0, 16),
    ((-2, 1), 0, 16),
)
READY = 2
GROUPS = (10, 6, 3, 2)
VMEM = pl.BlockSpec(memory_space=pltpu.VMEM)
ANY = pl.BlockSpec(memory_space=pl.ANY)
LIMIT = 4 * 1024 * 1024
WIDE = 50 * 1024 * 1024
HALF = (8, 8, 128)


def f32(*shape):
    return jax.ShapeDtypeStruct(shape, jnp.float32)


def bf16(*shape):
    return jax.ShapeDtypeStruct(shape, jnp.bfloat16)


def cost(elements, bytes_each):
    return pl.CostEstimate(flops=elements * 8, bytes_accessed=elements * bytes_each, transcendentals=0)


def there(offset):
    z, c = lax.axis_index("zero_0"), lax.axis_index("zero_1")
    return lax.rem(z + offset[0] + 8, 8), lax.rem(c + offset[1], 2)


def expert_of(start, core):
    return start if start >= 0 else core * 8 if start == OWN else (1 - core) * 8


def pick(piece, x_ref, out_ref, sem):
    offset, start, count = piece
    z, c = there(offset)
    first = pl.multiple_of((z * 2 + c) * 64, 64)
    expert = expert_of(start, lax.axis_index("zero_1"))
    return pltpu.make_async_copy(x_ref.at[pl.ds(expert, count), pl.ds(first, 64), :], out_ref, sem)


def pick_kernel(pieces, x_ref, *refs):
    copies = [pick(piece, x_ref, ref, refs[-1].at[i]) for i, (piece, ref) in enumerate(zip(pieces, refs))]
    for copy in copies:
        copy.start()
    for copy in copies:
        copy.wait()


def picked(pieces, x):
    return pl.pallas_call(
        functools.partial(pick_kernel, pieces),
        in_specs=[ANY],
        out_specs=[VMEM] * len(pieces),
        out_shape=[f32(piece[2], 64, 128) for piece in pieces],
        scratch_shapes=[pltpu.SemaphoreType.DMA((len(pieces),))],
        compiler_params=pltpu.CompilerParams(vmem_limit_bytes=WIDE),
        cost_estimate=cost(sum(piece[2] for piece in pieces) * 64 * 128, 8),
        name="pick",
    )(x)


def maxima_kernel(pieces, x_ref, keep_ref, give_ref, *refs):
    halves_ref, held_ref, sems, pick_sems = refs[len(pieces) :]
    experts = x_ref.shape[0]
    lane = lax.broadcasted_iota(jnp.int32, (8, 128), 1)

    def copy(e):
        return pltpu.make_async_copy(x_ref.at[e], held_ref.at[e], sems.at[e])

    for e in range(experts):
        copy(e).start()
    picks = [pick(piece, x_ref, ref, pick_sems.at[i]) for i, (piece, ref) in enumerate(zip(pieces, refs))]
    for each in picks:
        each.start()

    @pl.loop(0, experts // 4)
    def _(g):
        half, part = g // 2, lax.rem(g, 2)
        for e in range(4):
            copy(g * 4 + e).wait()
        for q in range(8):
            tile = jnp.where(part == 0, jnp.zeros((8, 128), jnp.float32), halves_ref[half, q])
            for j in range(2):
                for e in range(4):
                    for r in range(8):
                        row = (q * 2 + j) * 64 + r * 8
                        top = jnp.max(jnp.abs(held_ref[g * 4 + e, row : row + 8, :]), axis=1, keepdims=True)
                        tile = jnp.where(lane == j * 64 + (part * 4 + e) * 8 + r, top, tile)
            halves_ref[half, q] = tile

    low = lax.axis_index("zero_1") == 0
    keep_ref[...] = jnp.where(low, halves_ref[0], halves_ref[1])
    give_ref[...] = jnp.where(low, halves_ref[1], halves_ref[0])
    for each in picks:
        each.wait()


def local_maxima(x, pieces):
    return pl.pallas_call(
        functools.partial(maxima_kernel, pieces),
        in_specs=[ANY],
        out_specs=[VMEM] * (2 + len(pieces)),
        out_shape=[f32(*HALF), f32(*HALF)] + [f32(piece[2], 64, 128) for piece in pieces],
        scratch_shapes=[
            pltpu.VMEM((2, *HALF), jnp.float32),
            pltpu.VMEM(x.shape, jnp.float32),
            pltpu.SemaphoreType.DMA((x.shape[0],)),
            pltpu.SemaphoreType.DMA((len(pieces),)),
        ],
        compiler_params=pltpu.CompilerParams(vmem_limit_bytes=WIDE),
        name="local_maxima",
    )(x)


def chip_kernel(keep_ref, got_ref, weight_ref, gain_ref, out_ref):
    both = jnp.maximum(keep_ref[...], got_ref[...])
    router = weight_ref[...] * gain_ref[...]
    for q in range(8):
        out_ref[q, 0:8] = both
        out_ref[q, 8] = router[0:8]
        out_ref[q, 9] = router[8:16]


def chip_maxima(keep, got, weight, gain):
    return pl.pallas_call(
        chip_kernel,
        in_specs=[VMEM] * 4,
        out_specs=VMEM,
        out_shape=f32(8, 10, 8, 128),
        compiler_params=pltpu.CompilerParams(vmem_limit_bytes=LIMIT),
        name="chip",
    )(keep, got, weight, gain)


def joint_kernel(shared_ref, mine_ref, router_ref):
    top = shared_ref[0, 0:8]
    for q in range(1, 8):
        top = jnp.maximum(top, shared_ref[q, 0:8])
    mine_ref[...] = top
    for q in range(8):
        router_ref[q] = jnp.concatenate([shared_ref[q, 8], shared_ref[q, 9]], axis=0).astype(jnp.bfloat16)


def joined(shared):
    return pl.pallas_call(
        joint_kernel,
        in_specs=[VMEM],
        out_specs=[VMEM] * 2,
        out_shape=[f32(*HALF), bf16(8, 16, 128)],
        compiler_params=pltpu.CompilerParams(vmem_limit_bytes=LIMIT),
        name="joint",
    )(shared)


def route_kernel(mine_ref, their_ref, out_ref):
    low = lax.axis_index("zero_1") == 0
    for q in range(8):
        mine, theirs = mine_ref[q], their_ref[q]
        out_ref[:, q * 256 : q * 256 + 128] = jnp.where(low, mine, theirs)
        out_ref[:, q * 256 + 128 : q * 256 + 256] = jnp.where(low, theirs, mine)


def routed(mine, theirs):
    return pl.pallas_call(
        route_kernel,
        in_specs=[VMEM] * 2,
        out_specs=VMEM,
        out_shape=bf16(16, 2048),
        compiler_params=pltpu.CompilerParams(vmem_limit_bytes=LIMIT),
        name="route",
    )(mine, theirs)


def scales_at(refs, offset):
    z, c = there(offset)
    tiles = [ref[z] for ref in refs]
    return [jnp.where(c == 0, tile[:, 0:64], tile[:, 64:128]) for tile in tiles]


def scales_in_order(refs, offset):
    own, other = scales_at(refs, offset)
    low = lax.axis_index("zero_1") == 0
    return [jnp.where(low, own, other), jnp.where(low, other, own)]


def divide_rows(rows_ref, out_ref, scales, experts, start):
    for e in experts:
        scale = scales[(start + e) // 8]
        for r in range(0, 8, 2):
            lane = (start + e) % 8 * 8 + r
            both = jnp.concatenate([scale[:, lane : lane + 1], scale[:, lane + 1 : lane + 2]], axis=0)
            out_ref[e, r * 8 : r * 8 + 16, :] = (rows_ref[e, r * 8 : r * 8 + 16, :] / both).astype(jnp.bfloat16)


def ready_kernel(offset, rows_ref, mine_ref, out_ref):
    divide_rows(rows_ref, out_ref, scales_at([mine_ref], offset), range(8), 0)


def ready(piece, rows, mine):
    return pl.pallas_call(
        functools.partial(ready_kernel, piece[0]),
        in_specs=[VMEM, VMEM],
        out_specs=VMEM,
        out_shape=bf16(8, 64, 128),
        compiler_params=pltpu.CompilerParams(vmem_limit_bytes=LIMIT),
        cost_estimate=cost(8 * 64 * 128, 6),
        name="ready",
    )(rows, mine)


def divide_kernel(piece, x_ref, mine_ref, their_ref, out_ref, rows_ref, sems):
    offset, start, count = piece
    z, c = there(offset)
    first = pl.multiple_of((z * 2 + c) * 64, 64)
    expert = expert_of(start, lax.axis_index("zero_1"))
    parts = [range(e, min(e + 4, count)) for e in range(0, count, 4)]
    copies = [
        pltpu.make_async_copy(
            x_ref.at[pl.ds(expert + part[0], len(part)), pl.ds(first, 64), :],
            rows_ref.at[pl.ds(part[0], len(part))],
            sems.at[i],
        )
        for i, part in enumerate(parts)
    ]
    for copy in copies:
        copy.start()
    if start == OTHER:
        scales, start = scales_at([their_ref], offset), 0
    else:
        scales = scales_in_order([mine_ref, their_ref], offset)
    for copy, part in zip(copies, parts):
        copy.wait()
        divide_rows(rows_ref, out_ref, scales, part, start)


def divided(piece, x, mine, theirs):
    count = piece[2]
    return pl.pallas_call(
        functools.partial(divide_kernel, piece),
        in_specs=[ANY, VMEM, VMEM],
        out_specs=VMEM,
        out_shape=bf16(count, 64, 128),
        scratch_shapes=[pltpu.VMEM((count, 64, 128), jnp.float32), pltpu.SemaphoreType.DMA((pl.cdiv(count, 4),))],
        compiler_params=pltpu.CompilerParams(vmem_limit_bytes=WIDE),
        cost_estimate=cost(count * 64 * 128, 6),
        name="divide",
    )(x, mine, theirs)


def finish_kernel(pieces, *refs):
    n = len(pieces)
    rows, (mine_ref, their_ref), outs, (scale_ref, turned_ref) = refs[:n], refs[n : n + 2], refs[n + 2 : -2], refs[-2:]
    scales = scales_in_order([mine_ref, their_ref], (0, 0))
    for i, (_, start, count) in enumerate(pieces):
        divide_rows(rows[i], outs[i], scales, range(count), start)
    tile = jnp.concatenate(scales, axis=1)
    turned_ref[...] = jnp.concatenate([tile, jnp.zeros((120, 128), jnp.float32)], axis=0).T
    lane = lax.broadcasted_iota(jnp.int32, (16, 128), 1)
    out = turned_ref[pl.ds(0, 16, stride=8), :]
    for r in range(1, 8):
        part = pltpu.roll(turned_ref[pl.ds(r, 16, stride=8), :], r * 8, axis=1)
        out = jnp.where(lane >= r * 8, part, out)
    scale_ref[...] = out[:, 0:64]


def finished(pieces, rows, mine, theirs):
    n = len(pieces)
    return pl.pallas_call(
        functools.partial(finish_kernel, pieces),
        in_specs=[VMEM] * (n + 2),
        out_specs=[VMEM] * (n + 1),
        out_shape=[bf16(piece[2], 64, 128) for piece in pieces] + [f32(16, 64)],
        scratch_shapes=[pltpu.VMEM((128, 128), jnp.float32)],
        compiler_params=pltpu.CompilerParams(vmem_limit_bytes=LIMIT),
        cost_estimate=cost(sum(piece[2] for piece in pieces) * 64 * 128, 6),
        name="finish",
    )(*rows, mine, theirs)


def place_kernel(pieces, held, routed, *refs):
    n = len(pieces)
    blocks, refs = refs[:n], refs[n + held :]
    out_ref, sems = refs[routed], refs[-1]
    copies = []
    for i, (offset, start, count) in enumerate(pieces):
        z, c = there((-offset[0], offset[1]))
        column = pl.multiple_of((z * 2 + c) * 128, 128)
        target = out_ref.at[pl.ds(expert_of(start, c), count), :, pl.ds(column, 128)]
        copies.append(pltpu.make_async_copy(blocks[i], target, sems.at[i]))
    if routed:
        copies.append(pltpu.make_async_copy(refs[0], refs[2], sems.at[n]))
    for copy in copies:
        copy.start()
    for copy in copies:
        copy.wait()


def placed(pieces, blocks, shape, into=None, router=None):
    n, held, routed = len(pieces), int(into is not None), int(router is not None)
    return pl.pallas_call(
        functools.partial(place_kernel, tuple(pieces), held, routed),
        in_specs=[VMEM] * n + [ANY] * held + [VMEM] * routed,
        out_specs=[ANY] * (1 + routed),
        out_shape=[bf16(*shape)] + ([bf16(*router.shape)] if routed else []),
        scratch_shapes=[pltpu.SemaphoreType.DMA((n + routed,))],
        input_output_aliases={n: 0} if held else {},
        compiler_params=pltpu.CompilerParams(vmem_limit_bytes=LIMIT),
        cost_estimate=cost(sum(piece[2] for piece in pieces) * 64 * 128, 4),
        name="place",
    )(*blocks, *([into] if held else []), *([router] if routed else []))


def sent(piece, offset):
    pairs = [(z * 2 + c, ((z + offset[0]) % 8) * 2 + (c + offset[1]) % 2) for z in range(8) for c in range(2)]
    return lax.ppermute(piece, ZERO, pairs)


def swapped(value):
    return sent(value, (0, 1))


def per_device(train_down, router_weight, router_gain):
    experts = train_down.shape[0]
    rows = picked(RAW[:1], train_down)
    keep, give, *more = local_maxima(train_down, RAW[1:])
    raw = []
    for i, part in enumerate([*rows, *more]):
        raw.append(sent(part, RAW[i][0]))
    given = swapped(give)
    payload = chip_maxima(keep, given, router_weight.T, router_gain[None, :])
    shared = lax.all_to_all(payload, "zero_0", 0, 0, tiled=True)
    waiting = picked(PIECES[:READY], train_down)
    mine, lines = joined(shared)
    theirs = swapped(mine)

    kept = ((0, 0), 0, experts)
    blocks = []
    for i, piece in enumerate(PIECES):
        part = ready(piece, waiting[i], mine) if i < READY else divided(piece, train_down, mine, theirs)
        blocks.append(sent(part, piece[0]))

    lines = routed(lines, swapped(lines))
    lines, _ = lax.optimization_barrier((lines, blocks[2]))
    router = lax.all_gather(lines, "bank", axis=0, tiled=True)

    early = [divided(kept, train_down, mine, theirs)]
    *more, scale_down = finished(RAW, raw, mine, theirs)
    pieces, blocks = (kept,) + RAW + PIECES, [*early, *more, *blocks]
    shape = (experts, 64, 2048)
    ready_down, first = None, 0
    for i, n in enumerate(GROUPS):
        group = slice(first, first + n)
        out = placed(pieces[group], blocks[group], shape, ready_down, router if i == 1 else None)
        ready_down, first = out[0], first + n
        if i == 1:
            serve_router = out[1].T

    return (ready_down, scale_down, serve_router)


def solution(mesh):
    torus = Mesh(
        mesh.devices.reshape(mesh.shape["unit"], mesh.shape["bank"], 8, 2),
        ("unit", "bank", "zero_0", "zero_1"),
    )
    placed_at = (P(("unit", "bank"), None, ZERO), P(UNIT_ZERO, "bank"), P(UNIT_ZERO))
    return jax.shard_map(
        per_device,
        mesh=torus,
        in_specs=placed_at,
        out_specs=(P(("unit", "bank"), ZERO, None), P(("unit", "bank"), ZERO), P("unit", None)),
        check_vma=False,
    )
```

time: 159 us -> 138 us (0.87)
  blocking collectives: 28.5 us -> 12.4 us
  starting transfers between devices: 44.1 us -> 57.7 us
  local copies, waits for them, and re-layouts: 10.1 us -> 0.01 us
  waiting for transfers between devices: 36.5 us -> 29.8 us
    all_to_all x1 -> x0, blocking collectives: 16.2 us -> none  [exchanged(): return lax.all_to_all(value, ZERO, 0, 0, tiled=True)]
    ppermute x20 -> x23, waiting for transfers between devices: 36.5 us -> 26.3 us  [sent(): return lax.ppermute(piece, ZERO, pairs)]
    ppermute x20 -> x23, starting transfers between devices: 40.6 us -> 49.2 us  [sent(): return lax.ppermute(piece, ZERO, pairs)]
    unnamed x25 -> x4, local copies, waits for them, and re-layouts: 7.86 us -> 0.01 us
    all_to_all x1, starting transfers between devices: 3.52 us -> 8.47 us  [per_device(): shared = lax.all_to_all(payload, 'zero_0', 0, 0, tiled=True)]
    all_to_all x1, waiting for transfers between devices: 0.01 us -> 3.54 us  [per_device(): shared = lax.all_to_all(payload, 'zero_0', 0, 0, tiled=True)]
    pallas_call x7 -> x8, Pallas kernels: 2.59 us -> 4.36 us  [the longest x2 2.02 us: picked(): pl.pallas_call(functools.partial(pick_kernel, pieces), in_specs=[ANY], ou...]
    pallas_call x16, Pallas kernels: 24.5 us -> 22.8 us  [divided(): pl.pallas_call(functools.partial(divide_kernel, piece), in_specs=[ANY, VM...]
  transfers between devices with their start and end apart: 21 -> 24, of which waited for: 5 -> 9; matrix products, arithmetic and copies ran while one was open for 2% -> 0% of each run, Pallas kernels for 19% -> 22%
where the time goes in v1:
time: 138 us; the launch traced here: 137 us
  starting transfers between devices  57.7 us (42%)
  Pallas kernels  35.5 us (26%)
  waiting for transfers between devices  29.8 us (22%)
  blocking collectives  12.4 us (9%)
    ppermute x23, starting transfers between devices, sent(): return lax.ppermute(piece, ZERO, pairs)  49.2 us
    ppermute x23, waiting for transfers between devices, sent(): return lax.ppermute(piece, ZERO, pairs)  26.3 us
    pallas_call x16, Pallas kernels, divided(): pl.pallas_call(functools.partial(divide_kernel, piece), in_specs=[ANY, VM...  22.8 us
    all_gather x1, blocking collectives, per_device(): router = lax.all_gather(lines, 'bank', axis=0, tiled=True)  12.4 us
    all_to_all x1, starting transfers between devices, per_device(): shared = lax.all_to_all(payload, 'zero_0', 0, 0, tiled=True)  8.47 us
    pallas_call x1, Pallas kernels, local_maxima(): pl.pallas_call(functools.partial(maxima_kernel, pieces), in_specs=[ANY],...  4.22 us
    pallas_call x4, Pallas kernels, placed(): pl.pallas_call(functools.partial(place_kernel, tuple(pieces), held, route...  4.16 us
    all_to_all x1, waiting for transfers between devices, per_device(): shared = lax.all_to_all(payload, 'zero_0', 0, 0, tiled=True)  3.54 us
  transfers between devices with their start and end apart: 24, of which 9 were waited for; matrix products, arithmetic and copies ran while one was open for 0% of the time, Pallas kernels for 22%

profile of v1, /device:TPU:2, one launch (start us, length us, event | category | flops | bytes accessed | tf_op | source)
XLA Modules:
  0.0 136.6 jit_solution(14480549355432706977)
XLA Ops:
  0.7 4.2 %local_maxima.1 = (f32[8,8,128]{2,1,0:T(8,128)S(1)}, f32[8,8,128]{2,1,0:T(8,128)S(1)}, f32[5,64,128]{2,1,0:T(8,128)S(1)}, f32[7,64,128]{2,1,0:T(8,128)S(1)}) custom-call(f32[16,1024,128]{2,1,0:T(8,128)} %x_ref.37), custom_call_target="tpu_custom_call" | custom-call | tf_op jit(solution)/shard_map/local_maxima/pallas_call | solution.py:132
  6.9 8.5 %all-to-all-start = ((f32[8,10,8,128]{3,2,1,0:T(8,128)}), f32[8,10,8,128]{3,2,1,0:T(8,128)S(1)}, u32[]{:S(2)}, u32[]{:S(2)}) async-start(f32[8,10,8,128]{3,2,1,0:T(8,128)} %chip.1), calls=%async_computation | async-start | bytes 655360 | tf_op jit(solution)/shard_map/all_to_all | solution.py:364
  16.4 6.0 %collective-permute-start.13 = (f32[8,64,128]{2,1,0:T(8,128)S(1)}, f32[8,64,128]{2,1,0:T(8,128)S(1)}, u32[]{:S(2)}, u32[]{:S(2)}) collective-permute-start(f32[8,64,128]{2,1,0:T(8,128)S(1)} %pick.2), channel_id=1, source_target_pairs={{0,8},{1,9},{2,10},{3,11},{4,12},{5,13},{6,14},{7,15},{8,0},{9,1},... | collective-permute-start | bytes 786440 | tf_op jit(solution)/shard_map/ppermute | solution.py:348
  22.9 2.4 %collective-permute-start.14 = (f32[5,64,128]{2,1,0:T(8,128)S(1)}, f32[5,64,128]{2,1,0:T(8,128)S(1)}, u32[]{:S(2)}, u32[]{:S(2)}) collective-permute-start(f32[5,64,128]{2,1,0:T(8,128)S(1)} %get-tuple-element.21), channel_id=1, source_target_pairs={{0,4},{1,5},{2,6},{3,7},{4,8},{5,9},{6,10},{7,11},{8,12},{9,13},{1... | collective-permute-start | bytes 491528 | tf_op jit(solution)/shard_map/ppermute | solution.py:348
  25.3 3.5 %all-to-all-done.shared_ref = f32[8,10,8,128]{3,2,1,0:T(8,128)S(1)} async-done(((f32[8,10,8,128]{3,2,1,0:T(8,128)}), f32[8,10,8,128]{3,2,1,0:T(8,128)S(1)}, u32[]{:S(2)}, u32[]{:S(2)}) %all-to-all-start) | async-done | bytes 327712 | tf_op jit(solution)/shard_map/all_to_all | solution.py:364
  30.3 2.8 %collective-permute-start.16 = (bf16[8,64,128]{2,1,0:T(8,128)(2,1)S(1)}, bf16[8,64,128]{2,1,0:T(8,128)(2,1)S(1)}, u32[]{:S(2)}, u32[]{:S(2)}) collective-permute-start(bf16[8,64,128]{2,1,0:T(8,128)(2,1)S(1)} %ready.2), channel_id=1, source_target_pairs={{0,6},{1,7},{2,8},{3,9},{4,10},{5,11},{6,12},{7,13},{8,14},{9,15},... | collective-permute-start | bytes 393224 | tf_op jit(solution)/shard_map/ppermute | solution.py:348
  33.4 4.1 %collective-permute-start.17 = (bf16[8,64,128]{2,1,0:T(8,128)(2,1)S(1)}, bf16[8,64,128]{2,1,0:T(8,128)(2,1)S(1)}, u32[]{:S(2)}, u32[]{:S(2)}) collective-permute-start(bf16[8,64,128]{2,1,0:T(8,128)(2,1)S(1)} %ready.3), channel_id=1, source_target_pairs={{0,10},{1,11},{2,12},{3,13},{4,14},{5,15},{6,0},{7,1},{8,2},{9,3},... | collective-permute-start | bytes 393224 | tf_op jit(solution)/shard_map/ppermute | solution.py:348
  37.5 1.5 %divide.29 = bf16[16,64,128]{2,1,0:T(8,128)(2,1)S(1)} custom-call(f32[16,1024,128]{2,1,0:T(8,128)} %x_ref.37, f32[8,8,128]{2,1,0:T(8,128)S(1)} %get-tuple-element.20.mine_ref.refs_3_, f32[8,8,128]{2,1,0:T(8,128)S(1)} %collective-permute-done.1.their_ref.refs_4_), custom_call_target="tpu_custom_call" | custom-call | flops 1048576 | bytes 786432 | tf_op jit(solution)/shard_map/divide/pallas_call | solution.py:271
  38.9 8.9 %collective-permute-done.14.refs_1_ = f32[5,64,128]{2,1,0:T(8,128)S(1)} collective-permute-done((f32[5,64,128]{2,1,0:T(8,128)S(1)}, f32[5,64,128]{2,1,0:T(8,128)S(1)}, u32[]{:S(2)}, u32[]{:S(2)}) %collective-permute-start.14) | collective-permute-done | bytes 163872 | tf_op jit(solution)/shard_map/ppermute | solution.py:348
  48.4 1.5 %collective-permute-done.15.refs_2_ = f32[7,64,128]{2,1,0:T(8,128)S(1)} collective-permute-done((f32[7,64,128]{2,1,0:T(8,128)S(1)}, f32[7,64,128]{2,1,0:T(8,128)S(1)}, u32[]{:S(2)}, u32[]{:S(2)}) %collective-permute-start.15) | collective-permute-done | bytes 229408 | tf_op jit(solution)/shard_map/ppermute | solution.py:348
  49.9 1.5 %divide.30 = bf16[16,64,128]{2,1,0:T(8,128)(2,1)S(1)} custom-call(f32[16,1024,128]{2,1,0:T(8,128)} %x_ref.37, f32[8,8,128]{2,1,0:T(8,128)S(1)} %get-tuple-element.20.mine_ref.refs_3_, f32[8,8,128]{2,1,0:T(8,128)S(1)} %collective-permute-done.1.their_ref.refs_4_), custom_call_target="tpu_custom_call" | custom-call | flops 1048576 | bytes 786432 | tf_op jit(solution)/shard_map/divide/pallas_call | solution.py:271
  51.4 2.8 %collective-permute-start.20 = (bf16[16,64,128]{2,1,0:T(8,128)(2,1)S(1)}, bf16[16,64,128]{2,1,0:T(8,128)(2,1)S(1)}, u32[]{:S(2)}, u32[]{:S(2)}) collective-permute-start(bf16[16,64,128]{2,1,0:T(8,128)(2,1)S(1)} %divide.30), channel_id=1, source_target_pairs={{0,11},{1,10},{2,13},{3,12},{4,15},{5,14},{6,1},{7,0},{8,3},{9,2},... | collective-permute-start | bytes 786440 | tf_op jit(solution)/shard_map/ppermute | solution.py:348
  55.4 4.2 %collective-permute-start.18 = (bf16[8,64,128]{2,1,0:T(8,128)(2,1)S(1)}, bf16[8,64,128]{2,1,0:T(8,128)(2,1)S(1)}, u32[]{:S(2)}, u32[]{:S(2)}) collective-permute-start(bf16[8,64,128]{2,1,0:T(8,128)(2,1)S(1)} %divide.28), channel_id=1, source_target_pairs={{0,8},{1,9},{2,10},{3,11},{4,12},{5,13},{6,14},{7,15},{8,0},{9,1},... | collective-permute-start | bytes 393224 | tf_op jit(solution)/shard_map/ppermute | solution.py:348
  62.1 4.7 %collective-permute-start.10 = (bf16[8,64,128]{2,1,0:T(8,128)(2,1)S(1)}, bf16[8,64,128]{2,1,0:T(8,128)(2,1)S(1)}, u32[]{:S(2)}, u32[]{:S(2)}) collective-permute-start(bf16[8,64,128]{2,1,0:T(8,128)(2,1)S(1)} %divide.24), channel_id=1, source_target_pairs={{0,10},{1,11},{2,12},{3,13},{4,14},{5,15},{6,0},{7,1},{8,2},{9,3},... | collective-permute-start | bytes 393224 | tf_op jit(solution)/shard_map/ppermute | solution.py:348
  66.8 1.5 %divide.31 = bf16[16,64,128]{2,1,0:T(8,128)(2,1)S(1)} custom-call(f32[16,1024,128]{2,1,0:T(8,128)} %x_ref.37, f32[8,8,128]{2,1,0:T(8,128)S(1)} %get-tuple-element.20.mine_ref.refs_3_, f32[8,8,128]{2,1,0:T(8,128)S(1)} %collective-permute-done.1.their_ref.refs_4_), custom_call_target="tpu_custom_call" | custom-call | flops 1048576 | bytes 786432 | tf_op jit(solution)/shard_map/divide/pallas_call | solution.py:271
  68.3 7.6 %collective-permute-done.18.refs_6_ = bf16[8,64,128]{2,1,0:T(8,128)(2,1)S(1)} collective-permute-done((bf16[8,64,128]{2,1,0:T(8,128)(2,1)S(1)}, bf16[8,64,128]{2,1,0:T(8,128)(2,1)S(1)}, u32[]{:S(2)}, u32[]{:S(2)}) %collective-permute-start.18) | collective-permute-done | bytes 131104 | tf_op jit(solution)/shard_map/ppermute | solution.py:348
  75.9 7.6 %collective-permute-start.21 = (bf16[16,64,128]{2,1,0:T(8,128)(2,1)S(1)}, bf16[16,64,128]{2,1,0:T(8,128)(2,1)S(1)}, u32[]{:S(2)}, u32[]{:S(2)}) collective-permute-start(bf16[16,64,128]{2,1,0:T(8,128)(2,1)S(1)} %divide.31), channel_id=1, source_target_pairs={{0,2},{1,3},{2,4},{3,5},{4,6},{5,7},{6,8},{7,9},{8,10},{9,11},{10,... | collective-permute-start | bytes 786440 | tf_op jit(solution)/shard_map/ppermute | solution.py:348
  83.5 1.5 %divide.25 = bf16[16,64,128]{2,1,0:T(8,128)(2,1)S(1)} custom-call(f32[16,1024,128]{2,1,0:T(8,128)} %x_ref.37, f32[8,8,128]{2,1,0:T(8,128)S(1)} %get-tuple-element.20.mine_ref.refs_3_, f32[8,8,128]{2,1,0:T(8,128)S(1)} %collective-permute-done.1.their_ref.refs_4_), custom_call_target="tpu_custom_call" | custom-call | flops 1048576 | bytes 786432 | tf_op jit(solution)/shard_map/divide/pallas_call | solution.py:271
  85.0 1.5 %divide.26 = bf16[16,64,128]{2,1,0:T(8,128)(2,1)S(1)} custom-call(f32[16,1024,128]{2,1,0:T(8,128)} %x_ref.37, f32[8,8,128]{2,1,0:T(8,128)S(1)} %get-tuple-element.20.mine_ref.refs_3_, f32[8,8,128]{2,1,0:T(8,128)S(1)} %collective-permute-done.1.their_ref.refs_4_), custom_call_target="tpu_custom_call" | custom-call | flops 1048576 | bytes 786432 | tf_op jit(solution)/shard_map/divide/pallas_call | solution.py:271
  86.5 2.0 %collective-permute-done.10.refs_3_ = bf16[8,64,128]{2,1,0:T(8,128)(2,1)S(1)} collective-permute-done((bf16[8,64,128]{2,1,0:T(8,128)(2,1)S(1)}, bf16[8,64,128]{2,1,0:T(8,128)(2,1)S(1)}, u32[]{:S(2)}, u32[]{:S(2)}) %collective-permute-start.10) | collective-permute-done | bytes 131104 | tf_op jit(solution)/shard_map/ppermute | solution.py:348
  88.5 1.5 %divide.21 = bf16[16,64,128]{2,1,0:T(8,128)(2,1)S(1)} custom-call(f32[16,1024,128]{2,1,0:T(8,128)} %x_ref.37, f32[8,8,128]{2,1,0:T(8,128)S(1)} %get-tuple-element.20.mine_ref.refs_3_, f32[8,8,128]{2,1,0:T(8,128)S(1)} %collective-permute-done.1.their_ref.refs_4_), custom_call_target="tpu_custom_call" | custom-call | flops 1048576 | bytes 786432 | tf_op jit(solution)/shard_map/divide/pallas_call | solution.py:271
  90.0 3.4 %collective-permute-start.7 = (bf16[16,64,128]{2,1,0:T(8,128)(2,1)S(1)}, bf16[16,64,128]{2,1,0:T(8,128)(2,1)S(1)}, u32[]{:S(2)}, u32[]{:S(2)}) collective-permute-start(bf16[16,64,128]{2,1,0:T(8,128)(2,1)S(1)} %divide.21), channel_id=1, source_target_pairs={{0,14},{1,15},{2,0},{3,1},{4,2},{5,3},{6,4},{7,5},{8,6},{9,7},{10,... | collective-permute-start | bytes 786440 | tf_op jit(solution)/shard_map/ppermute | solution.py:348
  93.4 1.5 %divide.22 = bf16[16,64,128]{2,1,0:T(8,128)(2,1)S(1)} custom-call(f32[16,1024,128]{2,1,0:T(8,128)} %x_ref.37, f32[8,8,128]{2,1,0:T(8,128)S(1)} %get-tuple-element.20.mine_ref.refs_3_, f32[8,8,128]{2,1,0:T(8,128)S(1)} %collective-permute-done.1.their_ref.refs_4_), custom_call_target="tpu_custom_call" | custom-call | flops 1048576 | bytes 786432 | tf_op jit(solution)/shard_map/divide/pallas_call | solution.py:271
  94.9 1.7 %collective-permute-start.8 = (bf16[16,64,128]{2,1,0:T(8,128)(2,1)S(1)}, bf16[16,64,128]{2,1,0:T(8,128)(2,1)S(1)}, u32[]{:S(2)}, u32[]{:S(2)}) collective-permute-start(bf16[16,64,128]{2,1,0:T(8,128)(2,1)S(1)} %divide.22), channel_id=1, source_target_pairs={{0,9},{1,8},{2,11},{3,10},{4,13},{5,12},{6,15},{7,14},{8,1},{9,0},... | collective-permute-start | bytes 786440 | tf_op jit(solution)/shard_map/ppermute | solution.py:348
  96.7 1.5 %divide.18 = bf16[16,64,128]{2,1,0:T(8,128)(2,1)S(1)} custom-call(f32[16,1024,128]{2,1,0:T(8,128)} %x_ref.37, f32[8,8,128]{2,1,0:T(8,128)S(1)} %get-tuple-element.20.mine_ref.refs_3_, f32[8,8,128]{2,1,0:T(8,128)S(1)} %collective-permute-done.1.their_ref.refs_4_), custom_call_target="tpu_custom_call" | custom-call | flops 1048576 | bytes 786432 | tf_op jit(solution)/shard_map/divide/pallas_call | solution.py:271
  99.6 1.5 %divide.17 = bf16[16,64,128]{2,1,0:T(8,128)(2,1)S(1)} custom-call(f32[16,1024,128]{2,1,0:T(8,128)} %x_ref.37, f32[8,8,128]{2,1,0:T(8,128)S(1)} %get-tuple-element.20.mine_ref.refs_3_, f32[8,8,128]{2,1,0:T(8,128)S(1)} %collective-permute-done.1.their_ref.refs_4_), custom_call_target="tpu_custom_call" | custom-call | flops 1048576 | bytes 786432 | tf_op jit(solution)/shard_map/divide/pallas_call | solution.py:271
  101.1 1.5 %divide.16 = bf16[16,64,128]{2,1,0:T(8,128)(2,1)S(1)} custom-call(f32[16,1024,128]{2,1,0:T(8,128)} %x_ref.37, f32[8,8,128]{2,1,0:T(8,128)S(1)} %get-tuple-element.20.mine_ref.refs_3_, f32[8,8,128]{2,1,0:T(8,128)S(1)} %collective-permute-done.1.their_ref.refs_4_), custom_call_target="tpu_custom_call" | custom-call | flops 1048576 | bytes 786432 | tf_op jit(solution)/shard_map/divide/pallas_call | solution.py:271
  103.0 2.4 %collective-permute-start.2 = (bf16[16,64,128]{2,1,0:T(8,128)(2,1)S(1)}, bf16[16,64,128]{2,1,0:T(8,128)(2,1)S(1)}, u32[]{:S(2)}, u32[]{:S(2)}) collective-permute-start(bf16[16,64,128]{2,1,0:T(8,128)(2,1)S(1)} %divide.16), channel_id=1, source_target_pairs={{0,5},{1,4},{2,7},{3,6},{4,9},{5,8},{6,11},{7,10},{8,13},{9,12},{1... | collective-permute-start | bytes 786440 | tf_op jit(solution)/shard_map/ppermute | solution.py:348
  106.7 4.5 %collective-permute-done.7.refs_0_ = bf16[16,64,128]{2,1,0:T(8,128)(2,1)S(1)} collective-permute-done((bf16[16,64,128]{2,1,0:T(8,128)(2,1)S(1)}, bf16[16,64,128]{2,1,0:T(8,128)(2,1)S(1)}, u32[]{:S(2)}, u32[]{:S(2)}) %collective-permute-start.7) | collective-permute-done | bytes 262176 | tf_op jit(solution)/shard_map/ppermute | solution.py:348
  112.7 4.1 %collective-permute-start.6 = (bf16[9,64,128]{2,1,0:T(8,128)(2,1)S(1)}, bf16[9,64,128]{2,1,0:T(8,128)(2,1)S(1)}, u32[]{:S(2)}, u32[]{:S(2)}) collective-permute-start(bf16[9,64,128]{2,1,0:T(8,128)(2,1)S(1)} %divide.20), channel_id=1, source_target_pairs={{0,12},{1,13},{2,14},{3,15},{4,0},{5,1},{6,2},{7,3},{8,4},{9,5},{1... | collective-permute-start | bytes 442376 | tf_op jit(solution)/shard_map/ppermute | solution.py:348
  116.8 1.5 %divide.27.refs_0_ = bf16[16,64,128]{2,1,0:T(8,128)(2,1)S(1)} custom-call(f32[16,1024,128]{2,1,0:T(8,128)} %x_ref.37, f32[8,8,128]{2,1,0:T(8,128)S(1)} %get-tuple-element.20.mine_ref.refs_3_, f32[8,8,128]{2,1,0:T(8,128)S(1)} %collective-permute-done.1.their_ref.refs_4_), custom_call_target="tpu_custom_call" | custom-call | flops 1048576 | bytes 786432 | tf_op jit(solution)/shard_map/divide/pallas_call | solution.py:271
  119.3 12.4 %all_gather.3.refs_7_ = bf16[64,2048]{1,0:T(8,128)(2,1)S(1)} all-gather(bf16[16,2048]{1,0:T(8,128)(2,1)S(1)} %route.1), channel_id=1, replica_groups=mesh['unit'=4,'bank'=4,'zero_0'=8,'zero_1'=2] {'bank'}, dimensions={0}, use_global_device_ids=true | all-gather | bytes 327680 | tf_op jit(solution)/shard_map/all_gather | solution.py:377
  (50 shorter events, 19.8 us)
Async XLA Ops:
  0.6 5.5 %copy-start = (f32[128,16]{0,1:T(8,128)S(1)}, f32[128,16]{0,1:T(8,128)}, u32[]{:S(2)}) copy-start(f32[128,16]{0,1:T(8,128)} %param.4) | copy-start | bytes 24580
  0.6 5.5 %copy-start.1 = (f32[128]{0:T(128)S(1)}, f32[128]{0:T(128)}, u32[]{:S(2)}) copy-start(f32[128]{0:T(128)} %param.5) | copy-start | bytes 1540
  4.9 1.3 collective-permute-start
  6.9 21.9 %all-to-all-start = ((f32[8,10,8,128]{3,2,1,0:T(8,128)}), f32[8,10,8,128]{3,2,1,0:T(8,128)S(1)}, u32[]{:S(2)}, u32[]{:S(2)}) async-start(f32[8,10,8,128]{3,2,1,0:T(8,128)} %chip.1), calls=%async_computation | async-start | bytes 655360 | tf_op jit(solution)/shard_map/all_to_all | solution.py:364
  16.4 35.0 %collective-permute-start.13 = (f32[8,64,128]{2,1,0:T(8,128)S(1)}, f32[8,64,128]{2,1,0:T(8,128)S(1)}, u32[]{:S(2)}, u32[]{:S(2)}) collective-permute-start(f32[8,64,128]{2,1,0:T(8,128)S(1)} %pick.2), channel_id=1, source_target_pairs={{0,8},{1,9},{2,10},{3,11},{4,12},{5,13},{6,14},{7,15},{8,0},{9,1},... | collective-permute-start | bytes 786440 | tf_op jit(solution)/shard_map/ppermute | solution.py:348
  22.4 27.5 %collective-permute-start.15 = (f32[7,64,128]{2,1,0:T(8,128)S(1)}, f32[7,64,128]{2,1,0:T(8,128)S(1)}, u32[]{:S(2)}, u32[]{:S(2)}) collective-permute-start(f32[7,64,128]{2,1,0:T(8,128)S(1)} %get-tuple-element.22), channel_id=1, source_target_pairs={{0,12},{1,13},{2,14},{3,15},{4,0},{5,1},{6,2},{7,3},{8,4},{9,5},{1... | collective-permute-start | bytes 688136 | tf_op jit(solution)/shard_map/ppermute | solution.py:348
  22.9 24.9 %collective-permute-start.14 = (f32[5,64,128]{2,1,0:T(8,128)S(1)}, f32[5,64,128]{2,1,0:T(8,128)S(1)}, u32[]{:S(2)}, u32[]{:S(2)}) collective-permute-start(f32[5,64,128]{2,1,0:T(8,128)S(1)} %get-tuple-element.21), channel_id=1, source_target_pairs={{0,4},{1,5},{2,6},{3,7},{4,8},{5,9},{6,10},{7,11},{8,12},{9,13},{1... | collective-permute-start | bytes 491528 | tf_op jit(solution)/shard_map/ppermute | solution.py:348
  28.9 4.5 %collective-permute-start.1 = (f32[8,8,128]{2,1,0:T(8,128)S(1)}, f32[8,8,128]{2,1,0:T(8,128)S(1)}, u32[]{:S(2)}, u32[]{:S(2)}) collective-permute-start(f32[8,8,128]{2,1,0:T(8,128)S(1)} %get-tuple-element.20.mine_ref.refs_3_), channel_id=1, source_target_pairs={{0,1},{1,0},{2,3},{3,2},{4,5},{5,4},{6,7},{7,6},{8,9},{9,8},{10,11... | collective-permute-start | bytes 98312 | tf_op jit(solution)/shard_map/ppermute | solution.py:348
  30.3 31.8 %collective-permute-start.16 = (bf16[8,64,128]{2,1,0:T(8,128)(2,1)S(1)}, bf16[8,64,128]{2,1,0:T(8,128)(2,1)S(1)}, u32[]{:S(2)}, u32[]{:S(2)}) collective-permute-start(bf16[8,64,128]{2,1,0:T(8,128)(2,1)S(1)} %ready.2), channel_id=1, source_target_pairs={{0,6},{1,7},{2,8},{3,9},{4,10},{5,11},{6,12},{7,13},{8,14},{9,15},... | collective-permute-start | bytes 393224 | tf_op jit(solution)/shard_map/ppermute | solution.py:348
  33.4 33.4 %collective-permute-start.17 = (bf16[8,64,128]{2,1,0:T(8,128)(2,1)S(1)}, bf16[8,64,128]{2,1,0:T(8,128)(2,1)S(1)}, u32[]{:S(2)}, u32[]{:S(2)}) collective-permute-start(bf16[8,64,128]{2,1,0:T(8,128)(2,1)S(1)} %ready.3), channel_id=1, source_target_pairs={{0,10},{1,11},{2,12},{3,13},{4,14},{5,15},{6,0},{7,1},{8,2},{9,3},... | collective-permute-start | bytes 393224 | tf_op jit(solution)/shard_map/ppermute | solution.py:348
  47.9 42.2 %collective-permute-start.19 = (bf16[16,64,128]{2,1,0:T(8,128)(2,1)S(1)}, bf16[16,64,128]{2,1,0:T(8,128)(2,1)S(1)}, u32[]{:S(2)}, u32[]{:S(2)}) collective-permute-start(bf16[16,64,128]{2,1,0:T(8,128)(2,1)S(1)} %divide.29), channel_id=1, source_target_pairs={{0,7},{1,6},{2,9},{3,8},{4,11},{5,10},{6,13},{7,12},{8,15},{9,14},... | collective-permute-start | bytes 786440 | tf_op jit(solution)/shard_map/ppermute | solution.py:348
  49.9 5.5 %collective-permute-start.22 = (bf16[8,16,128]{2,1,0:T(8,128)(2,1)S(1)}, bf16[8,16,128]{2,1,0:T(8,128)(2,1)S(1)}, u32[]{:S(2)}, u32[]{:S(2)}) collective-permute-start(bf16[8,16,128]{2,1,0:T(8,128)(2,1)S(1)} %get-tuple-element.28.mine_ref), channel_id=1, source_target_pairs={{0,1},{1,0},{2,3},{3,2},{4,5},{5,4},{6,7},{7,6},{8,9},{9,8},{10,11... | collective-permute-start | bytes 98312 | tf_op jit(solution)/shard_map/ppermute | solution.py:348
  51.4 43.5 %collective-permute-start.20 = (bf16[16,64,128]{2,1,0:T(8,128)(2,1)S(1)}, bf16[16,64,128]{2,1,0:T(8,128)(2,1)S(1)}, u32[]{:S(2)}, u32[]{:S(2)}) collective-permute-start(bf16[16,64,128]{2,1,0:T(8,128)(2,1)S(1)} %divide.30), channel_id=1, source_target_pairs={{0,11},{1,10},{2,13},{3,12},{4,15},{5,14},{6,1},{7,0},{8,3},{9,2},... | collective-permute-start | bytes 786440 | tf_op jit(solution)/shard_map/ppermute | solution.py:348
  55.4 20.4 %collective-permute-start.18 = (bf16[8,64,128]{2,1,0:T(8,128)(2,1)S(1)}, bf16[8,64,128]{2,1,0:T(8,128)(2,1)S(1)}, u32[]{:S(2)}, u32[]{:S(2)}) collective-permute-start(bf16[8,64,128]{2,1,0:T(8,128)(2,1)S(1)} %divide.28), channel_id=1, source_target_pairs={{0,8},{1,9},{2,10},{3,11},{4,12},{5,13},{6,14},{7,15},{8,0},{9,1},... | collective-permute-start | bytes 393224 | tf_op jit(solution)/shard_map/ppermute | solution.py:348
  62.1 26.4 %collective-permute-start.10 = (bf16[8,64,128]{2,1,0:T(8,128)(2,1)S(1)}, bf16[8,64,128]{2,1,0:T(8,128)(2,1)S(1)}, u32[]{:S(2)}, u32[]{:S(2)}) collective-permute-start(bf16[8,64,128]{2,1,0:T(8,128)(2,1)S(1)} %divide.24), channel_id=1, source_target_pairs={{0,10},{1,11},{2,12},{3,13},{4,14},{5,15},{6,0},{7,1},{8,2},{9,3},... | collective-permute-start | bytes 393224 | tf_op jit(solution)/shard_map/ppermute | solution.py:348
  66.8 21.7 %collective-permute-start.9 = (bf16[8,64,128]{2,1,0:T(8,128)(2,1)S(1)}, bf16[8,64,128]{2,1,0:T(8,128)(2,1)S(1)}, u32[]{:S(2)}, u32[]{:S(2)}) collective-permute-start(bf16[8,64,128]{2,1,0:T(8,128)(2,1)S(1)} %divide.23), channel_id=1, source_target_pairs={{0,6},{1,7},{2,8},{3,9},{4,10},{5,11},{6,12},{7,13},{8,14},{9,15},... | collective-permute-start | bytes 393224 | tf_op jit(solution)/shard_map/ppermute | solution.py:348
  75.9 22.3 %collective-permute-start.21 = (bf16[16,64,128]{2,1,0:T(8,128)(2,1)S(1)}, bf16[16,64,128]{2,1,0:T(8,128)(2,1)S(1)}, u32[]{:S(2)}, u32[]{:S(2)}) collective-permute-start(bf16[16,64,128]{2,1,0:T(8,128)(2,1)S(1)} %divide.31), channel_id=1, source_target_pairs={{0,2},{1,3},{2,4},{3,5},{4,6},{5,7},{6,8},{7,9},{8,10},{9,11},{10,... | collective-permute-start | bytes 786440 | tf_op jit(solution)/shard_map/ppermute | solution.py:348
  88.5 14.2 %collective-permute-start.11 = (bf16[16,64,128]{2,1,0:T(8,128)(2,1)S(1)}, bf16[16,64,128]{2,1,0:T(8,128)(2,1)S(1)}, u32[]{:S(2)}, u32[]{:S(2)}) collective-permute-start(bf16[16,64,128]{2,1,0:T(8,128)(2,1)S(1)} %divide.25), channel_id=1, source_target_pairs={{0,1},{1,0},{2,3},{3,2},{4,5},{5,4},{6,7},{7,6},{8,9},{9,8},{10,11... | collective-permute-start | bytes 786440 | tf_op jit(solution)/shard_map/ppermute | solution.py:348
  88.5 14.5 %collective-permute-start.12 = (bf16[16,64,128]{2,1,0:T(8,128)(2,1)S(1)}, bf16[16,64,128]{2,1,0:T(8,128)(2,1)S(1)}, u32[]{:S(2)}, u32[]{:S(2)}) collective-permute-start(bf16[16,64,128]{2,1,0:T(8,128)(2,1)S(1)} %divide.26), channel_id=1, source_target_pairs={{0,3},{1,2},{2,5},{3,4},{4,7},{5,6},{6,9},{7,8},{8,11},{9,10},{10,... | collective-permute-start | bytes 786440 | tf_op jit(solution)/shard_map/ppermute | solution.py:348
  90.0 21.2 %collective-permute-start.7 = (bf16[16,64,128]{2,1,0:T(8,128)(2,1)S(1)}, bf16[16,64,128]{2,1,0:T(8,128)(2,1)S(1)}, u32[]{:S(2)}, u32[]{:S(2)}) collective-permute-start(bf16[16,64,128]{2,1,0:T(8,128)(2,1)S(1)} %divide.21), channel_id=1, source_target_pairs={{0,14},{1,15},{2,0},{3,1},{4,2},{5,3},{6,4},{7,5},{8,6},{9,7},{10,... | collective-permute-start | bytes 786440 | tf_op jit(solution)/shard_map/ppermute | solution.py:348
  94.9 17.8 %collective-permute-start.8 = (bf16[16,64,128]{2,1,0:T(8,128)(2,1)S(1)}, bf16[16,64,128]{2,1,0:T(8,128)(2,1)S(1)}, u32[]{:S(2)}, u32[]{:S(2)}) collective-permute-start(bf16[16,64,128]{2,1,0:T(8,128)(2,1)S(1)} %divide.22), channel_id=1, source_target_pairs={{0,9},{1,8},{2,11},{3,10},{4,13},{5,12},{6,15},{7,14},{8,1},{9,0},... | collective-permute-start | bytes 786440 | tf_op jit(solution)/shard_map/ppermute | solution.py:348
  98.2 36.5 %collective-permute-start.4 = (bf16[16,64,128]{2,1,0:T(8,128)(2,1)S(1)}, bf16[16,64,128]{2,1,0:T(8,128)(2,1)S(1)}, u32[]{:S(2)}, u32[]{:S(2)}) collective-permute-start(bf16[16,64,128]{2,1,0:T(8,128)(2,1)S(1)} %divide.18), channel_id=1, source_target_pairs={{0,15},{1,14},{2,1},{3,0},{4,3},{5,2},{6,5},{7,4},{8,7},{9,6},{10,... | collective-permute-start | bytes 786440 | tf_op jit(solution)/shard_map/ppermute | solution.py:348
  102.7 32.9 %collective-permute-start.3 = (bf16[16,64,128]{2,1,0:T(8,128)(2,1)S(1)}, bf16[16,64,128]{2,1,0:T(8,128)(2,1)S(1)}, u32[]{:S(2)}, u32[]{:S(2)}) collective-permute-start(bf16[16,64,128]{2,1,0:T(8,128)(2,1)S(1)} %divide.17), channel_id=1, source_target_pairs={{0,13},{1,12},{2,15},{3,14},{4,1},{5,0},{6,3},{7,2},{8,5},{9,4},{1... | collective-permute-start | bytes 786440 | tf_op jit(solution)/shard_map/ppermute | solution.py:348
  103.0 32.6 %collective-permute-start.2 = (bf16[16,64,128]{2,1,0:T(8,128)(2,1)S(1)}, bf16[16,64,128]{2,1,0:T(8,128)(2,1)S(1)}, u32[]{:S(2)}, u32[]{:S(2)}) collective-permute-start(bf16[16,64,128]{2,1,0:T(8,128)(2,1)S(1)} %divide.16), channel_id=1, source_target_pairs={{0,5},{1,4},{2,7},{3,6},{4,9},{5,8},{6,11},{7,10},{8,13},{9,12},{1... | collective-permute-start | bytes 786440 | tf_op jit(solution)/shard_map/ppermute | solution.py:348
  111.2 23.5 %collective-permute-start.5 = (bf16[11,64,128]{2,1,0:T(8,128)(2,1)S(1)}, bf16[11,64,128]{2,1,0:T(8,128)(2,1)S(1)}, u32[]{:S(2)}, u32[]{:S(2)}) collective-permute-start(bf16[11,64,128]{2,1,0:T(8,128)(2,1)S(1)} %divide.19), channel_id=1, source_target_pairs={{0,4},{1,5},{2,6},{3,7},{4,8},{5,9},{6,10},{7,11},{8,12},{9,13},{1... | collective-permute-start | bytes 540680 | tf_op jit(solution)/shard_map/ppermute | solution.py:348
  112.7 22.0 %collective-permute-start.6 = (bf16[9,64,128]{2,1,0:T(8,128)(2,1)S(1)}, bf16[9,64,128]{2,1,0:T(8,128)(2,1)S(1)}, u32[]{:S(2)}, u32[]{:S(2)}) collective-permute-start(bf16[9,64,128]{2,1,0:T(8,128)(2,1)S(1)} %divide.20), channel_id=1, source_target_pairs={{0,12},{1,13},{2,14},{3,15},{4,0},{5,1},{6,2},{7,3},{8,4},{9,5},{1... | collective-permute-start | bytes 442376 | tf_op jit(solution)/shard_map/ppermute | solution.py:348

commit v2 on v1

--- a/solution.py
+++ b/solution.py
@@ -13,7 +13,8 @@
 UNIT_ZERO = ("unit", "zero_0", "zero_1")
 
 OWN, OTHER = -1, -2
-RAW = (((4, 0), 0, 8), ((2, 0), 0, 5), ((-2, 0), 0, 7))
+RAW = (((4, 0), 0, 8), ((2, 0), 0, 10))
+EARLY = 1
 PIECES = (
     ((3, 0), OWN, 8),
     ((-3, 0), OWN, 8),
@@ -26,15 +27,15 @@
     ((3, 0), OTHER, 8),
     ((-3, 0), OTHER, 8),
     ((0, 1), 0, 16),
+    ((2, 0), 10, 6),
+    ((-2, 0), 0, 16),
     ((1, 1), 0, 16),
     ((-1, 1), 0, 16),
-    ((2, 0), 5, 11),
-    ((-2, 0), 7, 9),
     ((2, 1), 0, 16),
     ((-2, 1), 0, 16),
 )
 READY = 2
-GROUPS = (10, 6, 3, 2)
+GROUPS = (9, 6, 3, 2)
 VMEM = pl.BlockSpec(memory_space=pltpu.VMEM)
 ANY = pl.BlockSpec(memory_space=pl.ANY)
 LIMIT = 4 * 1024 * 1024
@@ -54,9 +55,18 @@
     return pl.CostEstimate(flops=elements * 8, bytes_accessed=elements * bytes_each, transcendentals=0)
 
 
+def way(core):
+    return 1 - 2 * core
+
+
 def there(offset):
     z, c = lax.axis_index("zero_0"), lax.axis_index("zero_1")
-    return lax.rem(z + offset[0] + 8, 8), lax.rem(c + offset[1], 2)
+    return lax.rem(z + way(c) * offset[0] + 8, 8), lax.rem(c + offset[1], 2)
+
+
+def sender(offset):
+    c = lax.rem(lax.axis_index("zero_1") + offset[1], 2)
+    return lax.rem(lax.axis_index("zero_0") - way(c) * offset[0] + 8, 8), c
 
 
 def expert_of(start, core):
@@ -316,7 +326,7 @@
     out_ref, sems = refs[routed], refs[-1]
     copies = []
     for i, (offset, start, count) in enumerate(pieces):
-        z, c = there((-offset[0], offset[1]))
+        z, c = sender(offset)
         column = pl.multiple_of((z * 2 + c) * 128, 128)
         target = out_ref.at[pl.ds(expert_of(start, c), count), :, pl.ds(column, 128)]
         copies.append(pltpu.make_async_copy(blocks[i], target, sems.at[i]))
@@ -344,7 +354,7 @@
 
 
 def sent(piece, offset):
-    pairs = [(z * 2 + c, ((z + offset[0]) % 8) * 2 + (c + offset[1]) % 2) for z in range(8) for c in range(2)]
+    pairs = [(z * 2 + c, (z + way(c) * offset[0]) % 8 * 2 + (c + offset[1]) % 2) for z in range(8) for c in range(2)]
     return lax.ppermute(piece, ZERO, pairs)
 
 
@@ -354,8 +364,8 @@
 
 def per_device(train_down, router_weight, router_gain):
     experts = train_down.shape[0]
-    rows = picked(RAW[:1], train_down)
-    keep, give, *more = local_maxima(train_down, RAW[1:])
+    rows = picked(RAW[:EARLY], train_down)
+    keep, give, *more = local_maxima(train_down, RAW[EARLY:])
     raw = []
     for i, part in enumerate([*rows, *more]):
         raw.append(sent(part, RAW[i][0]))

time: 138 us -> 134 us (0.971)
  the two profiles are of different devices: /device:TPU:2 before, /device:TPU:1 now
where the time goes in v2:
time: 134 us
  starting transfers between devices  72.2 us (54%)
  Pallas kernels  35.6 us (27%)
  waiting for transfers between devices  14.4 us (11%)
  blocking collectives  10.3 us (8%)
    ppermute x22, starting transfers between devices, sent(): return lax.ppermute(piece, ZERO, pairs)  65.7 us
    pallas_call x16, Pallas kernels, divided(): pl.pallas_call(functools.partial(divide_kernel, piece), in_specs=[ANY, VM...  22.9 us
    all_gather x1, blocking collectives, per_device(): router = lax.all_gather(lines, 'bank', axis=0, tiled=True)  10.3 us
    ppermute x22, waiting for transfers between devices, sent(): return lax.ppermute(piece, ZERO, pairs)  7.82 us
    all_to_all x1, waiting for transfers between devices, per_device(): shared = lax.all_to_all(payload, 'zero_0', 0, 0, tiled=True)  6.54 us
    all_to_all x1, starting transfers between devices, per_device(): shared = lax.all_to_all(payload, 'zero_0', 0, 0, tiled=True)  6.48 us
    pallas_call x1, Pallas kernels, local_maxima(): pl.pallas_call(functools.partial(maxima_kernel, pieces), in_specs=[ANY],...  4.18 us
    pallas_call x4, Pallas kernels, placed(): pl.pallas_call(functools.partial(place_kernel, tuple(pieces), held, route...  4.18 us
  transfers between devices with their start and end apart: 23, of which 5 were waited for; matrix products, arithmetic and copies ran while one was open for 0% of the time, Pallas kernels for 22%

profile of v2, /device:TPU:1, one launch (start us, length us, event | category | flops | bytes accessed | tf_op | source)
XLA Modules:
  0.0 133.6 jit_solution(2869499391374742635)
XLA Ops:
  0.7 4.2 %local_maxima.1 = (f32[8,8,128]{2,1,0:T(8,128)S(1)}, f32[8,8,128]{2,1,0:T(8,128)S(1)}, f32[10,64,128]{2,1,0:T(8,128)S(1)}) custom-call(f32[16,1024,128]{2,1,0:T(8,128)} %x_ref.37), custom_call_target="tpu_custom_call" | custom-call | tf_op jit(solution)/shard_map/local_maxima/pallas_call | solution.py:142
  4.8 3.3 %collective-permute-start = (f32[8,8,128]{2,1,0:T(8,128)S(1)}, f32[8,8,128]{2,1,0:T(8,128)S(1)}, u32[]{:S(2)}, u32[]{:S(2)}) collective-permute-start(f32[8,8,128]{2,1,0:T(8,128)S(1)} %get-tuple-element.17), channel_id=1, source_target_pairs={{0,1},{1,0},{2,3},{3,2},{4,5},{5,4},{6,7},{7,6},{8,9},{9,8},{10,11... | collective-permute-start | bytes 98312 | tf_op jit(solution)/shard_map/ppermute | solution.py:358
  9.7 6.5 %all-to-all-start = ((f32[8,10,8,128]{3,2,1,0:T(8,128)}), f32[8,10,8,128]{3,2,1,0:T(8,128)S(1)}, u32[]{:S(2)}, u32[]{:S(2)}) async-start(f32[8,10,8,128]{3,2,1,0:T(8,128)} %chip.1), calls=%async_computation | async-start | bytes 655360 | tf_op jit(solution)/shard_map/all_to_all | solution.py:374
  16.2 3.6 %collective-permute-start.14 = (f32[10,64,128]{2,1,0:T(8,128)S(1)}, f32[10,64,128]{2,1,0:T(8,128)S(1)}, u32[]{:S(2)}, u32[]{:S(2)}) collective-permute-start(f32[10,64,128]{2,1,0:T(8,128)S(1)} %get-tuple-element.19), channel_id=1, source_target_pairs={{0,4},{1,13},{2,6},{3,15},{4,8},{5,1},{6,10},{7,3},{8,12},{9,5},{1... | collective-permute-start | bytes 983048 | tf_op jit(solution)/shard_map/ppermute | solution.py:358
  20.8 2.2 %collective-permute-start.13 = (f32[8,64,128]{2,1,0:T(8,128)S(1)}, f32[8,64,128]{2,1,0:T(8,128)S(1)}, u32[]{:S(2)}, u32[]{:S(2)}) collective-permute-start(f32[8,64,128]{2,1,0:T(8,128)S(1)} %pick.2), channel_id=1, source_target_pairs={{0,8},{1,9},{2,10},{3,11},{4,12},{5,13},{6,14},{7,15},{8,0},{9,1},... | collective-permute-start | bytes 786440 | tf_op jit(solution)/shard_map/ppermute | solution.py:358
  22.9 6.5 %all-to-all-done.shared_ref = f32[8,10,8,128]{3,2,1,0:T(8,128)S(1)} async-done(((f32[8,10,8,128]{3,2,1,0:T(8,128)}), f32[8,10,8,128]{3,2,1,0:T(8,128)S(1)}, u32[]{:S(2)}, u32[]{:S(2)}) %all-to-all-start) | async-done | bytes 327712 | tf_op jit(solution)/shard_map/all_to_all | solution.py:374
  29.5 1.5 %collective-permute-start.1 = (f32[8,8,128]{2,1,0:T(8,128)S(1)}, f32[8,8,128]{2,1,0:T(8,128)S(1)}, u32[]{:S(2)}, u32[]{:S(2)}) collective-permute-start(f32[8,8,128]{2,1,0:T(8,128)S(1)} %get-tuple-element.18.mine_ref.refs_2_), channel_id=1, source_target_pairs={{0,1},{1,0},{2,3},{3,2},{4,5},{5,4},{6,7},{7,6},{8,9},{9,8},{10,11... | collective-permute-start | bytes 98312 | tf_op jit(solution)/shard_map/ppermute | solution.py:358
  32.3 2.3 %collective-permute-start.15 = (bf16[8,64,128]{2,1,0:T(8,128)(2,1)S(1)}, bf16[8,64,128]{2,1,0:T(8,128)(2,1)S(1)}, u32[]{:S(2)}, u32[]{:S(2)}) collective-permute-start(bf16[8,64,128]{2,1,0:T(8,128)(2,1)S(1)} %ready.2), channel_id=1, source_target_pairs={{0,6},{1,11},{2,8},{3,13},{4,10},{5,15},{6,12},{7,1},{8,14},{9,3},... | collective-permute-start | bytes 393224 | tf_op jit(solution)/shard_map/ppermute | solution.py:358
  34.6 1.5 %divide.29 = bf16[16,64,128]{2,1,0:T(8,128)(2,1)S(1)} custom-call(f32[16,1024,128]{2,1,0:T(8,128)} %x_ref.37, f32[8,8,128]{2,1,0:T(8,128)S(1)} %get-tuple-element.18.mine_ref.refs_2_, f32[8,8,128]{2,1,0:T(8,128)S(1)} %collective-permute-done.1.their_ref.refs_3_), custom_call_target="tpu_custom_call" | custom-call | flops 1048576 | bytes 786432 | tf_op jit(solution)/shard_map/divide/pallas_call | solution.py:281
  36.1 2.6 %collective-permute-start.18 = (bf16[16,64,128]{2,1,0:T(8,128)(2,1)S(1)}, bf16[16,64,128]{2,1,0:T(8,128)(2,1)S(1)}, u32[]{:S(2)}, u32[]{:S(2)}) collective-permute-start(bf16[16,64,128]{2,1,0:T(8,128)(2,1)S(1)} %divide.29), channel_id=1, source_target_pairs={{0,7},{1,10},{2,9},{3,12},{4,11},{5,14},{6,13},{7,0},{8,15},{9,2},... | collective-permute-start | bytes 786440 | tf_op jit(solution)/shard_map/ppermute | solution.py:358
  41.2 13.3 %collective-permute-start.21 = (bf16[8,16,128]{2,1,0:T(8,128)(2,1)S(1)}, bf16[8,16,128]{2,1,0:T(8,128)(2,1)S(1)}, u32[]{:S(2)}, u32[]{:S(2)}) collective-permute-start(bf16[8,16,128]{2,1,0:T(8,128)(2,1)S(1)} %get-tuple-element.24.mine_ref), channel_id=1, source_target_pairs={{0,1},{1,0},{2,3},{3,2},{4,5},{5,4},{6,7},{7,6},{8,9},{9,8},{10,11... | collective-permute-start | bytes 98312 | tf_op jit(solution)/shard_map/ppermute | solution.py:358
  58.4 4.5 %collective-permute-start.9 = (bf16[8,64,128]{2,1,0:T(8,128)(2,1)S(1)}, bf16[8,64,128]{2,1,0:T(8,128)(2,1)S(1)}, u32[]{:S(2)}, u32[]{:S(2)}) collective-permute-start(bf16[8,64,128]{2,1,0:T(8,128)(2,1)S(1)} %divide.23), channel_id=1, source_target_pairs={{0,6},{1,11},{2,8},{3,13},{4,10},{5,15},{6,12},{7,1},{8,14},{9,3},... | collective-permute-start | bytes 393224 | tf_op jit(solution)/shard_map/ppermute | solution.py:358
  64.2 4.2 %collective-permute-start.12 = (bf16[6,64,128]{2,1,0:T(8,128)(2,1)S(1)}, bf16[6,64,128]{2,1,0:T(8,128)(2,1)S(1)}, u32[]{:S(2)}, u32[]{:S(2)}) collective-permute-start(bf16[6,64,128]{2,1,0:T(8,128)(2,1)S(1)} %divide.26), channel_id=1, source_target_pairs={{0,4},{1,13},{2,6},{3,15},{4,8},{5,1},{6,10},{7,3},{8,12},{9,5},{1... | collective-permute-start | bytes 294920 | tf_op jit(solution)/shard_map/ppermute | solution.py:358
  68.3 1.5 %divide.30 = bf16[16,64,128]{2,1,0:T(8,128)(2,1)S(1)} custom-call(f32[16,1024,128]{2,1,0:T(8,128)} %x_ref.37, f32[8,8,128]{2,1,0:T(8,128)S(1)} %get-tuple-element.18.mine_ref.refs_2_, f32[8,8,128]{2,1,0:T(8,128)S(1)} %collective-permute-done.1.their_ref.refs_3_), custom_call_target="tpu_custom_call" | custom-call | flops 1048576 | bytes 786432 | tf_op jit(solution)/shard_map/divide/pallas_call | solution.py:281
  69.8 1.5 %divide.31 = bf16[16,64,128]{2,1,0:T(8,128)(2,1)S(1)} custom-call(f32[16,1024,128]{2,1,0:T(8,128)} %x_ref.37, f32[8,8,128]{2,1,0:T(8,128)S(1)} %get-tuple-element.18.mine_ref.refs_2_, f32[8,8,128]{2,1,0:T(8,128)S(1)} %collective-permute-done.1.their_ref.refs_3_), custom_call_target="tpu_custom_call" | custom-call | flops 1048576 | bytes 786432 | tf_op jit(solution)/shard_map/divide/pallas_call | solution.py:281
  71.3 1.5 %divide.25 = bf16[16,64,128]{2,1,0:T(8,128)(2,1)S(1)} custom-call(f32[16,1024,128]{2,1,0:T(8,128)} %x_ref.37, f32[8,8,128]{2,1,0:T(8,128)S(1)} %get-tuple-element.18.mine_ref.refs_2_, f32[8,8,128]{2,1,0:T(8,128)S(1)} %collective-permute-done.1.their_ref.refs_3_), custom_call_target="tpu_custom_call" | custom-call | flops 1048576 | bytes 786432 | tf_op jit(solution)/shard_map/divide/pallas_call | solution.py:281
  72.8 5.0 %collective-permute-done.12.refs_5_ = bf16[6,64,128]{2,1,0:T(8,128)(2,1)S(1)} collective-permute-done((bf16[6,64,128]{2,1,0:T(8,128)(2,1)S(1)}, bf16[6,64,128]{2,1,0:T(8,128)(2,1)S(1)}, u32[]{:S(2)}, u32[]{:S(2)}) %collective-permute-start.12) | collective-permute-done | bytes 98336 | tf_op jit(solution)/shard_map/ppermute | solution.py:358
  78.8 2.8 %collective-permute-start.20 = (bf16[16,64,128]{2,1,0:T(8,128)(2,1)S(1)}, bf16[16,64,128]{2,1,0:T(8,128)(2,1)S(1)}, u32[]{:S(2)}, u32[]{:S(2)}) collective-permute-start(bf16[16,64,128]{2,1,0:T(8,128)(2,1)S(1)} %divide.31), channel_id=1, source_target_pairs={{0,2},{1,15},{2,4},{3,1},{4,6},{5,3},{6,8},{7,5},{8,10},{9,7},{10,... | collective-permute-start | bytes 786440 | tf_op jit(solution)/shard_map/ppermute | solution.py:358
  82.3 1.5 %divide.21 = bf16[16,64,128]{2,1,0:T(8,128)(2,1)S(1)} custom-call(f32[16,1024,128]{2,1,0:T(8,128)} %x_ref.37, f32[8,8,128]{2,1,0:T(8,128)S(1)} %get-tuple-element.18.mine_ref.refs_2_, f32[8,8,128]{2,1,0:T(8,128)S(1)} %collective-permute-done.1.their_ref.refs_3_), custom_call_target="tpu_custom_call" | custom-call | flops 1048576 | bytes 786432 | tf_op jit(solution)/shard_map/divide/pallas_call | solution.py:281
  83.8 1.5 %divide.22 = bf16[16,64,128]{2,1,0:T(8,128)(2,1)S(1)} custom-call(f32[16,1024,128]{2,1,0:T(8,128)} %x_ref.37, f32[8,8,128]{2,1,0:T(8,128)S(1)} %get-tuple-element.18.mine_ref.refs_2_, f32[8,8,128]{2,1,0:T(8,128)S(1)} %collective-permute-done.1.their_ref.refs_3_), custom_call_target="tpu_custom_call" | custom-call | flops 1048576 | bytes 786432 | tf_op jit(solution)/shard_map/divide/pallas_call | solution.py:281
  85.4 5.0 %collective-permute-start.8 = (bf16[16,64,128]{2,1,0:T(8,128)(2,1)S(1)}, bf16[16,64,128]{2,1,0:T(8,128)(2,1)S(1)}, u32[]{:S(2)}, u32[]{:S(2)}) collective-permute-start(bf16[16,64,128]{2,1,0:T(8,128)(2,1)S(1)} %divide.22), channel_id=1, source_target_pairs={{0,9},{1,8},{2,11},{3,10},{4,13},{5,12},{6,15},{7,14},{8,1},{9,0},... | collective-permute-start | bytes 786440 | tf_op jit(solution)/shard_map/ppermute | solution.py:358
  90.4 1.5 %divide.18 = bf16[16,64,128]{2,1,0:T(8,128)(2,1)S(1)} custom-call(f32[16,1024,128]{2,1,0:T(8,128)} %x_ref.37, f32[8,8,128]{2,1,0:T(8,128)S(1)} %get-tuple-element.18.mine_ref.refs_2_, f32[8,8,128]{2,1,0:T(8,128)S(1)} %collective-permute-done.1.their_ref.refs_3_), custom_call_target="tpu_custom_call" | custom-call | flops 1048576 | bytes 786432 | tf_op jit(solution)/shard_map/divide/pallas_call | solution.py:281
  91.9 1.5 %divide.19 = bf16[16,64,128]{2,1,0:T(8,128)(2,1)S(1)} custom-call(f32[16,1024,128]{2,1,0:T(8,128)} %x_ref.37, f32[8,8,128]{2,1,0:T(8,128)S(1)} %get-tuple-element.18.mine_ref.refs_2_, f32[8,8,128]{2,1,0:T(8,128)S(1)} %collective-permute-done.1.their_ref.refs_3_), custom_call_target="tpu_custom_call" | custom-call | flops 1048576 | bytes 786432 | tf_op jit(solution)/shard_map/divide/pallas_call | solution.py:281
  93.4 1.5 %divide.20 = bf16[16,64,128]{2,1,0:T(8,128)(2,1)S(1)} custom-call(f32[16,1024,128]{2,1,0:T(8,128)} %x_ref.37, f32[8,8,128]{2,1,0:T(8,128)S(1)} %get-tuple-element.18.mine_ref.refs_2_, f32[8,8,128]{2,1,0:T(8,128)S(1)} %collective-permute-done.1.their_ref.refs_3_), custom_call_target="tpu_custom_call" | custom-call | flops 1048576 | bytes 786432 | tf_op jit(solution)/shard_map/divide/pallas_call | solution.py:281
  95.0 2.6 %collective-permute-start.4 = (bf16[16,64,128]{2,1,0:T(8,128)(2,1)S(1)}, bf16[16,64,128]{2,1,0:T(8,128)(2,1)S(1)}, u32[]{:S(2)}, u32[]{:S(2)}) collective-permute-start(bf16[16,64,128]{2,1,0:T(8,128)(2,1)S(1)} %divide.18), channel_id=1, source_target_pairs={{0,12},{1,5},{2,14},{3,7},{4,0},{5,9},{6,2},{7,11},{8,4},{9,13},{1... | collective-permute-start | bytes 786440 | tf_op jit(solution)/shard_map/ppermute | solution.py:358
  97.6 1.8 %collective-permute-start.6 = (bf16[16,64,128]{2,1,0:T(8,128)(2,1)S(1)}, bf16[16,64,128]{2,1,0:T(8,128)(2,1)S(1)}, u32[]{:S(2)}, u32[]{:S(2)}) collective-permute-start(bf16[16,64,128]{2,1,0:T(8,128)(2,1)S(1)} %divide.20), channel_id=1, source_target_pairs={{0,15},{1,2},{2,1},{3,4},{4,3},{5,6},{6,5},{7,8},{8,7},{9,10},{10,... | collective-permute-start | bytes 786440 | tf_op jit(solution)/shard_map/ppermute | solution.py:358
  99.4 1.5 %divide.17 = bf16[16,64,128]{2,1,0:T(8,128)(2,1)S(1)} custom-call(f32[16,1024,128]{2,1,0:T(8,128)} %x_ref.37, f32[8,8,128]{2,1,0:T(8,128)S(1)} %get-tuple-element.18.mine_ref.refs_2_, f32[8,8,128]{2,1,0:T(8,128)S(1)} %collective-permute-done.1.their_ref.refs_3_), custom_call_target="tpu_custom_call" | custom-call | flops 1048576 | bytes 786432 | tf_op jit(solution)/shard_map/divide/pallas_call | solution.py:281
  100.9 1.5 %divide.16 = bf16[16,64,128]{2,1,0:T(8,128)(2,1)S(1)} custom-call(f32[16,1024,128]{2,1,0:T(8,128)} %x_ref.37, f32[8,8,128]{2,1,0:T(8,128)S(1)} %get-tuple-element.18.mine_ref.refs_2_, f32[8,8,128]{2,1,0:T(8,128)S(1)} %collective-permute-done.1.their_ref.refs_3_), custom_call_target="tpu_custom_call" | custom-call | flops 1048576 | bytes 786432 | tf_op jit(solution)/shard_map/divide/pallas_call | solution.py:281
  102.4 3.0 %collective-permute-start.3 = (bf16[16,64,128]{2,1,0:T(8,128)(2,1)S(1)}, bf16[16,64,128]{2,1,0:T(8,128)(2,1)S(1)}, u32[]{:S(2)}, u32[]{:S(2)}) collective-permute-start(bf16[16,64,128]{2,1,0:T(8,128)(2,1)S(1)} %divide.17), channel_id=1, source_target_pairs={{0,13},{1,4},{2,15},{3,6},{4,1},{5,8},{6,3},{7,10},{8,5},{9,12},{1... | collective-permute-start | bytes 786440 | tf_op jit(solution)/shard_map/ppermute | solution.py:358
  106.3 10.0 %collective-permute-start.2 = (bf16[16,64,128]{2,1,0:T(8,128)(2,1)S(1)}, bf16[16,64,128]{2,1,0:T(8,128)(2,1)S(1)}, u32[]{:S(2)}, u32[]{:S(2)}) collective-permute-start(bf16[16,64,128]{2,1,0:T(8,128)(2,1)S(1)} %divide.16), channel_id=1, source_target_pairs={{0,5},{1,12},{2,7},{3,14},{4,9},{5,0},{6,11},{7,2},{8,13},{9,4},{1... | collective-permute-start | bytes 786440 | tf_op jit(solution)/shard_map/ppermute | solution.py:358
  116.3 1.5 %divide.27.refs_0_ = bf16[16,64,128]{2,1,0:T(8,128)(2,1)S(1)} custom-call(f32[16,1024,128]{2,1,0:T(8,128)} %x_ref.37, f32[8,8,128]{2,1,0:T(8,128)S(1)} %get-tuple-element.18.mine_ref.refs_2_, f32[8,8,128]{2,1,0:T(8,128)S(1)} %collective-permute-done.1.their_ref.refs_3_), custom_call_target="tpu_custom_call" | custom-call | flops 1048576 | bytes 786432 | tf_op jit(solution)/shard_map/divide/pallas_call | solution.py:281
  118.9 10.3 %all_gather.3.refs_7_ = bf16[64,2048]{1,0:T(8,128)(2,1)S(1)} all-gather(bf16[16,2048]{1,0:T(8,128)(2,1)S(1)} %route.1), channel_id=1, replica_groups=mesh['unit'=4,'bank'=4,'zero_0'=8,'zero_1'=2] {'bank'}, dimensions={0}, use_global_device_ids=true | all-gather | bytes 327680 | tf_op jit(solution)/shard_map/all_gather | solution.py:387
  (48 shorter events, 19.4 us)
Async XLA Ops:
  0.6 8.4 %copy-start = (f32[128,16]{0,1:T(8,128)S(1)}, f32[128,16]{0,1:T(8,128)}, u32[]{:S(2)}) copy-start(f32[128,16]{0,1:T(8,128)} %param.4) | copy-start | bytes 24580
  0.6 8.3 %copy-start.1 = (f32[128]{0:T(128)S(1)}, f32[128]{0:T(128)}, u32[]{:S(2)}) copy-start(f32[128]{0:T(128)} %param.5) | copy-start | bytes 1540
  4.8 4.1 %collective-permute-start = (f32[8,8,128]{2,1,0:T(8,128)S(1)}, f32[8,8,128]{2,1,0:T(8,128)S(1)}, u32[]{:S(2)}, u32[]{:S(2)}) collective-permute-start(f32[8,8,128]{2,1,0:T(8,128)S(1)} %get-tuple-element.17), channel_id=1, source_target_pairs={{0,1},{1,0},{2,3},{3,2},{4,5},{5,4},{6,7},{7,6},{8,9},{9,8},{10,11... | collective-permute-start | bytes 98312 | tf_op jit(solution)/shard_map/ppermute | solution.py:358
  9.7 19.7 %all-to-all-start = ((f32[8,10,8,128]{3,2,1,0:T(8,128)}), f32[8,10,8,128]{3,2,1,0:T(8,128)S(1)}, u32[]{:S(2)}, u32[]{:S(2)}) async-start(f32[8,10,8,128]{3,2,1,0:T(8,128)} %chip.1), calls=%async_computation | async-start | bytes 655360 | tf_op jit(solution)/shard_map/all_to_all | solution.py:374
  16.2 40.7 %collective-permute-start.14 = (f32[10,64,128]{2,1,0:T(8,128)S(1)}, f32[10,64,128]{2,1,0:T(8,128)S(1)}, u32[]{:S(2)}, u32[]{:S(2)}) collective-permute-start(f32[10,64,128]{2,1,0:T(8,128)S(1)} %get-tuple-element.19), channel_id=1, source_target_pairs={{0,4},{1,13},{2,6},{3,15},{4,8},{5,1},{6,10},{7,3},{8,12},{9,5},{1... | collective-permute-start | bytes 983048 | tf_op jit(solution)/shard_map/ppermute | solution.py:358
  20.8 20.5 %collective-permute-start.13 = (f32[8,64,128]{2,1,0:T(8,128)S(1)}, f32[8,64,128]{2,1,0:T(8,128)S(1)}, u32[]{:S(2)}, u32[]{:S(2)}) collective-permute-start(f32[8,64,128]{2,1,0:T(8,128)S(1)} %pick.2), channel_id=1, source_target_pairs={{0,8},{1,9},{2,10},{3,11},{4,12},{5,13},{6,14},{7,15},{8,0},{9,1},... | collective-permute-start | bytes 786440 | tf_op jit(solution)/shard_map/ppermute | solution.py:358
  29.5 5.1 %collective-permute-start.1 = (f32[8,8,128]{2,1,0:T(8,128)S(1)}, f32[8,8,128]{2,1,0:T(8,128)S(1)}, u32[]{:S(2)}, u32[]{:S(2)}) collective-permute-start(f32[8,8,128]{2,1,0:T(8,128)S(1)} %get-tuple-element.18.mine_ref.refs_2_), channel_id=1, source_target_pairs={{0,1},{1,0},{2,3},{3,2},{4,5},{5,4},{6,7},{7,6},{8,9},{9,8},{10,11... | collective-permute-start | bytes 98312 | tf_op jit(solution)/shard_map/ppermute | solution.py:358
  32.3 26.1 %collective-permute-start.15 = (bf16[8,64,128]{2,1,0:T(8,128)(2,1)S(1)}, bf16[8,64,128]{2,1,0:T(8,128)(2,1)S(1)}, u32[]{:S(2)}, u32[]{:S(2)}) collective-permute-start(bf16[8,64,128]{2,1,0:T(8,128)(2,1)S(1)} %ready.2), channel_id=1, source_target_pairs={{0,6},{1,11},{2,8},{3,13},{4,10},{5,15},{6,12},{7,1},{8,14},{9,3},... | collective-permute-start | bytes 393224 | tf_op jit(solution)/shard_map/ppermute | solution.py:358
  36.1 49.3 %collective-permute-start.18 = (bf16[16,64,128]{2,1,0:T(8,128)(2,1)S(1)}, bf16[16,64,128]{2,1,0:T(8,128)(2,1)S(1)}, u32[]{:S(2)}, u32[]{:S(2)}) collective-permute-start(bf16[16,64,128]{2,1,0:T(8,128)(2,1)S(1)} %divide.29), channel_id=1, source_target_pairs={{0,7},{1,10},{2,9},{3,12},{4,11},{5,14},{6,13},{7,0},{8,15},{9,2},... | collective-permute-start | bytes 786440 | tf_op jit(solution)/shard_map/ppermute | solution.py:358
  38.9 25.2 %collective-permute-start.16 = (bf16[8,64,128]{2,1,0:T(8,128)(2,1)S(1)}, bf16[8,64,128]{2,1,0:T(8,128)(2,1)S(1)}, u32[]{:S(2)}, u32[]{:S(2)}) collective-permute-start(bf16[8,64,128]{2,1,0:T(8,128)(2,1)S(1)} %ready.3), channel_id=1, source_target_pairs={{0,10},{1,7},{2,12},{3,9},{4,14},{5,11},{6,0},{7,13},{8,2},{9,15},... | collective-permute-start | bytes 393224 | tf_op jit(solution)/shard_map/ppermute | solution.py:358
  41.2 15.8 %collective-permute-start.21 = (bf16[8,16,128]{2,1,0:T(8,128)(2,1)S(1)}, bf16[8,16,128]{2,1,0:T(8,128)(2,1)S(1)}, u32[]{:S(2)}, u32[]{:S(2)}) collective-permute-start(bf16[8,16,128]{2,1,0:T(8,128)(2,1)S(1)} %get-tuple-element.24.mine_ref), channel_id=1, source_target_pairs={{0,1},{1,0},{2,3},{3,2},{4,5},{5,4},{6,7},{7,6},{8,9},{9,8},{10,11... | collective-permute-start | bytes 98312 | tf_op jit(solution)/shard_map/ppermute | solution.py:358
  57.0 21.8 %collective-permute-start.17 = (bf16[8,64,128]{2,1,0:T(8,128)(2,1)S(1)}, bf16[8,64,128]{2,1,0:T(8,128)(2,1)S(1)}, u32[]{:S(2)}, u32[]{:S(2)}) collective-permute-start(bf16[8,64,128]{2,1,0:T(8,128)(2,1)S(1)} %divide.28), channel_id=1, source_target_pairs={{0,8},{1,9},{2,10},{3,11},{4,12},{5,13},{6,14},{7,15},{8,0},{9,1},... | collective-permute-start | bytes 393224 | tf_op jit(solution)/shard_map/ppermute | solution.py:358
  57.1 24.5 %collective-permute-start.10 = (bf16[8,64,128]{2,1,0:T(8,128)(2,1)S(1)}, bf16[8,64,128]{2,1,0:T(8,128)(2,1)S(1)}, u32[]{:S(2)}, u32[]{:S(2)}) collective-permute-start(bf16[8,64,128]{2,1,0:T(8,128)(2,1)S(1)} %divide.24), channel_id=1, source_target_pairs={{0,10},{1,7},{2,12},{3,9},{4,14},{5,11},{6,0},{7,13},{8,2},{9,15},... | collective-permute-start | bytes 393224 | tf_op jit(solution)/shard_map/ppermute | solution.py:358
  58.4 26.9 %collective-permute-start.9 = (bf16[8,64,128]{2,1,0:T(8,128)(2,1)S(1)}, bf16[8,64,128]{2,1,0:T(8,128)(2,1)S(1)}, u32[]{:S(2)}, u32[]{:S(2)}) collective-permute-start(bf16[8,64,128]{2,1,0:T(8,128)(2,1)S(1)} %divide.23), channel_id=1, source_target_pairs={{0,6},{1,11},{2,8},{3,13},{4,10},{5,15},{6,12},{7,1},{8,14},{9,3},... | collective-permute-start | bytes 393224 | tf_op jit(solution)/shard_map/ppermute | solution.py:358
  64.2 13.7 %collective-permute-start.12 = (bf16[6,64,128]{2,1,0:T(8,128)(2,1)S(1)}, bf16[6,64,128]{2,1,0:T(8,128)(2,1)S(1)}, u32[]{:S(2)}, u32[]{:S(2)}) collective-permute-start(bf16[6,64,128]{2,1,0:T(8,128)(2,1)S(1)} %divide.26), channel_id=1, source_target_pairs={{0,4},{1,13},{2,6},{3,15},{4,8},{5,1},{6,10},{7,3},{8,12},{9,5},{1... | collective-permute-start | bytes 294920 | tf_op jit(solution)/shard_map/ppermute | solution.py:358
  77.8 17.1 %collective-permute-start.19 = (bf16[16,64,128]{2,1,0:T(8,128)(2,1)S(1)}, bf16[16,64,128]{2,1,0:T(8,128)(2,1)S(1)}, u32[]{:S(2)}, u32[]{:S(2)}) collective-permute-start(bf16[16,64,128]{2,1,0:T(8,128)(2,1)S(1)} %divide.30), channel_id=1, source_target_pairs={{0,11},{1,6},{2,13},{3,8},{4,15},{5,10},{6,1},{7,12},{8,3},{9,14},... | collective-permute-start | bytes 786440 | tf_op jit(solution)/shard_map/ppermute | solution.py:358
  78.8 18.8 %collective-permute-start.20 = (bf16[16,64,128]{2,1,0:T(8,128)(2,1)S(1)}, bf16[16,64,128]{2,1,0:T(8,128)(2,1)S(1)}, u32[]{:S(2)}, u32[]{:S(2)}) collective-permute-start(bf16[16,64,128]{2,1,0:T(8,128)(2,1)S(1)} %divide.31), channel_id=1, source_target_pairs={{0,2},{1,15},{2,4},{3,1},{4,6},{5,3},{6,8},{7,5},{8,10},{9,7},{10,... | collective-permute-start | bytes 786440 | tf_op jit(solution)/shard_map/ppermute | solution.py:358
  81.6 16.0 %collective-permute-start.11 = (bf16[16,64,128]{2,1,0:T(8,128)(2,1)S(1)}, bf16[16,64,128]{2,1,0:T(8,128)(2,1)S(1)}, u32[]{:S(2)}, u32[]{:S(2)}) collective-permute-start(bf16[16,64,128]{2,1,0:T(8,128)(2,1)S(1)} %divide.25), channel_id=1, source_target_pairs={{0,1},{1,0},{2,3},{3,2},{4,5},{5,4},{6,7},{7,6},{8,9},{9,8},{10,11... | collective-permute-start | bytes 786440 | tf_op jit(solution)/shard_map/ppermute | solution.py:358
  85.3 17.1 %collective-permute-start.7 = (bf16[16,64,128]{2,1,0:T(8,128)(2,1)S(1)}, bf16[16,64,128]{2,1,0:T(8,128)(2,1)S(1)}, u32[]{:S(2)}, u32[]{:S(2)}) collective-permute-start(bf16[16,64,128]{2,1,0:T(8,128)(2,1)S(1)} %divide.21), channel_id=1, source_target_pairs={{0,14},{1,3},{2,0},{3,5},{4,2},{5,7},{6,4},{7,9},{8,6},{9,11},{10,... | collective-permute-start | bytes 786440 | tf_op jit(solution)/shard_map/ppermute | solution.py:358
  85.4 20.9 %collective-permute-start.8 = (bf16[16,64,128]{2,1,0:T(8,128)(2,1)S(1)}, bf16[16,64,128]{2,1,0:T(8,128)(2,1)S(1)}, u32[]{:S(2)}, u32[]{:S(2)}) collective-permute-start(bf16[16,64,128]{2,1,0:T(8,128)(2,1)S(1)} %divide.22), channel_id=1, source_target_pairs={{0,9},{1,8},{2,11},{3,10},{4,13},{5,12},{6,15},{7,14},{8,1},{9,0},... | collective-permute-start | bytes 786440 | tf_op jit(solution)/shard_map/ppermute | solution.py:358
  95.0 36.6 %collective-permute-start.4 = (bf16[16,64,128]{2,1,0:T(8,128)(2,1)S(1)}, bf16[16,64,128]{2,1,0:T(8,128)(2,1)S(1)}, u32[]{:S(2)}, u32[]{:S(2)}) collective-permute-start(bf16[16,64,128]{2,1,0:T(8,128)(2,1)S(1)} %divide.18), channel_id=1, source_target_pairs={{0,12},{1,5},{2,14},{3,7},{4,0},{5,9},{6,2},{7,11},{8,4},{9,13},{1... | collective-permute-start | bytes 786440 | tf_op jit(solution)/shard_map/ppermute | solution.py:358
  97.6 34.0 %collective-permute-start.5 = (bf16[16,64,128]{2,1,0:T(8,128)(2,1)S(1)}, bf16[16,64,128]{2,1,0:T(8,128)(2,1)S(1)}, u32[]{:S(2)}, u32[]{:S(2)}) collective-permute-start(bf16[16,64,128]{2,1,0:T(8,128)(2,1)S(1)} %divide.19), channel_id=1, source_target_pairs={{0,3},{1,14},{2,5},{3,0},{4,7},{5,2},{6,9},{7,4},{8,11},{9,6},{10,... | collective-permute-start | bytes 786440 | tf_op jit(solution)/shard_map/ppermute | solution.py:358
  97.6 34.0 %collective-permute-start.6 = (bf16[16,64,128]{2,1,0:T(8,128)(2,1)S(1)}, bf16[16,64,128]{2,1,0:T(8,128)(2,1)S(1)}, u32[]{:S(2)}, u32[]{:S(2)}) collective-permute-start(bf16[16,64,128]{2,1,0:T(8,128)(2,1)S(1)} %divide.20), channel_id=1, source_target_pairs={{0,15},{1,2},{2,1},{3,4},{4,3},{5,6},{6,5},{7,8},{8,7},{9,10},{10,... | collective-permute-start | bytes 786440 | tf_op jit(solution)/shard_map/ppermute | solution.py:358
  102.4 30.2 %collective-permute-start.3 = (bf16[16,64,128]{2,1,0:T(8,128)(2,1)S(1)}, bf16[16,64,128]{2,1,0:T(8,128)(2,1)S(1)}, u32[]{:S(2)}, u32[]{:S(2)}) collective-permute-start(bf16[16,64,128]{2,1,0:T(8,128)(2,1)S(1)} %divide.17), channel_id=1, source_target_pairs={{0,13},{1,4},{2,15},{3,6},{4,1},{5,8},{6,3},{7,10},{8,5},{9,12},{1... | collective-permute-start | bytes 786440 | tf_op jit(solution)/shard_map/ppermute | solution.py:358
  106.3 26.3 %collective-permute-start.2 = (bf16[16,64,128]{2,1,0:T(8,128)(2,1)S(1)}, bf16[16,64,128]{2,1,0:T(8,128)(2,1)S(1)}, u32[]{:S(2)}, u32[]{:S(2)}) collective-permute-start(bf16[16,64,128]{2,1,0:T(8,128)(2,1)S(1)} %divide.16), channel_id=1, source_target_pairs={{0,5},{1,12},{2,7},{3,14},{4,9},{5,0},{6,11},{7,2},{8,13},{9,4},{1... | collective-permute-start | bytes 786440 | tf_op jit(solution)/shard_map/ppermute | solution.py:358

commit v3 on v2

--- a/solution.py
+++ b/solution.py
@@ -13,7 +13,7 @@
 UNIT_ZERO = ("unit", "zero_0", "zero_1")
 
 OWN, OTHER = -1, -2
-RAW = (((4, 0), 0, 8), ((2, 0), 0, 10))
+RAW = (((4, 0), 0, 8), ((2, 0), 0, 8))
 EARLY = 1
 PIECES = (
     ((3, 0), OWN, 8),
@@ -23,12 +23,12 @@
     ((-3, 1), 0, 16),
     ((1, 0), 0, 16),
     ((-1, 0), 0, 16),
+    ((-2, 0), 0, 16),
     ((4, 1), 0, 16),
     ((3, 0), OTHER, 8),
     ((-3, 0), OTHER, 8),
     ((0, 1), 0, 16),
-    ((2, 0), 10, 6),
-    ((-2, 0), 0, 16),
+    ((2, 0), 8, 8),
     ((1, 1), 0, 16),
     ((-1, 1), 0, 16),
     ((2, 1), 0, 16),
@@ -36,6 +36,7 @@
 )
 READY = 2
 GROUPS = (9, 6, 3, 2)
+CARRY = tuple(next(p for p in RAW[EARLY:] + PIECES if p[0] == (z, 0)) for z in (1, 2, 3, 4, -3, -2, -1))
 VMEM = pl.BlockSpec(memory_space=pltpu.VMEM)
 ANY = pl.BlockSpec(memory_space=pl.ANY)
 LIMIT = 4 * 1024 * 1024
@@ -73,36 +74,74 @@
     return start if start >= 0 else core * 8 if start == OWN else (1 - core) * 8
 
 
-def pick(piece, x_ref, out_ref, sem):
+def rows_of(piece):
+    return (piece[2] * 64 + 16, 128) if piece in CARRY else (piece[2], 64, 128)
+
+
+def expert_rows(ref, piece, e, first=0, count=64):
+    return ref.at[pl.ds(e * 64 + first, count)] if piece in CARRY else ref.at[e, pl.ds(first, count)]
+
+
+def tail_of(piece):
+    return pl.ds(piece[2] * 64, 16)
+
+
+def copies_of(piece):
+    return piece[2] if piece in CARRY else 1
+
+
+def pick(piece, x_ref, out_ref, sems, at):
     offset, start, count = piece
     z, c = there(offset)
-    first = pl.multiple_of((z * 2 + c) * 64, 64)
+    rows = pl.ds(pl.multiple_of((z * 2 + c) * 64, 64), 64)
     expert = expert_of(start, lax.axis_index("zero_1"))
-    return pltpu.make_async_copy(x_ref.at[pl.ds(expert, count), pl.ds(first, 64), :], out_ref, sem)
+    if piece not in CARRY:
+        return [pltpu.make_async_copy(x_ref.at[pl.ds(expert, count), rows, :], out_ref, sems.at[at])]
+    return [
+        pltpu.make_async_copy(x_ref.at[expert + e, rows, :], expert_rows(out_ref, piece, e), sems.at[at + e])
+        for e in range(count)
+    ]
+
+
+def picks(pieces, x_ref, refs, sems):
+    copies = []
+    for piece, ref in zip(pieces, refs):
+        copies += pick(piece, x_ref, ref, sems, len(copies))
+    return copies
 
 
 def pick_kernel(pieces, x_ref, *refs):
-    copies = [pick(piece, x_ref, ref, refs[-1].at[i]) for i, (piece, ref) in enumerate(zip(pieces, refs))]
+    routed = any(piece in CARRY for piece in pieces)
+    given, outs, rest = refs[: 2 * routed], refs[2 * routed : 2 * routed + len(pieces)], refs[2 * routed + len(pieces) :]
+    sems = rest[-1]
+    copies = picks(pieces, x_ref, outs, sems)
+    for source, target in zip(given, rest):
+        copies.append(pltpu.make_async_copy(source, target, sems.at[len(copies)]))
     for copy in copies:
         copy.start()
     for copy in copies:
         copy.wait()
-
-
-def picked(pieces, x):
+    for piece, ref in zip(pieces, outs):
+        if piece in CARRY:
+            ref[tail_of(piece), :] = rest[0][...] * rest[1][...]
+
+
+def picked(pieces, x, weight, gain):
+    more = [weight, gain] if any(piece in CARRY for piece in pieces) else []
     return pl.pallas_call(
         functools.partial(pick_kernel, pieces),
-        in_specs=[ANY],
+        in_specs=[ANY] * (1 + len(more)),
         out_specs=[VMEM] * len(pieces),
-        out_shape=[f32(piece[2], 64, 128) for piece in pieces],
-        scratch_shapes=[pltpu.SemaphoreType.DMA((len(pieces),))],
+        out_shape=[f32(*rows_of(piece)) for piece in pieces],
+        scratch_shapes=[pltpu.VMEM(each.shape, jnp.float32) for each in more]
+        + [pltpu.SemaphoreType.DMA((sum(copies_of(piece) for piece in pieces) + len(more),))],
         compiler_params=pltpu.CompilerParams(vmem_limit_bytes=WIDE),
         cost_estimate=cost(sum(piece[2] for piece in pieces) * 64 * 128, 8),
         name="pick",
-    )(x)
-
-
-def maxima_kernel(pieces, x_ref, keep_ref, give_ref, *refs):
+    )(x, *more)
+
+
+def maxima_kernel(pieces, x_ref, weight_ref, gain_ref, keep_ref, give_ref, *refs):
     halves_ref, held_ref, sems, pick_sems = refs[len(pieces) :]
     experts = x_ref.shape[0]
     lane = lax.broadcasted_iota(jnp.int32, (8, 128), 1)
@@ -112,9 +151,13 @@
 
     for e in range(experts):
         copy(e).start()
-    picks = [pick(piece, x_ref, ref, pick_sems.at[i]) for i, (piece, ref) in enumerate(zip(pieces, refs))]
-    for each in picks:
+    more = picks(pieces, x_ref, refs, pick_sems)
+    for each in more:
         each.start()
+    router = weight_ref[...] * gain_ref[...]
+    for piece, ref in zip(pieces, refs):
+        if piece in CARRY:
+            ref[tail_of(piece), :] = router
 
     @pl.loop(0, experts // 4)
     def _(g):
@@ -134,65 +177,78 @@
     low = lax.axis_index("zero_1") == 0
     keep_ref[...] = jnp.where(low, halves_ref[0], halves_ref[1])
     give_ref[...] = jnp.where(low, halves_ref[1], halves_ref[0])
-    for each in picks:
+    for each in more:
         each.wait()
 
 
-def local_maxima(x, pieces):
+def local_maxima(x, pieces, weight, gain):
     return pl.pallas_call(
         functools.partial(maxima_kernel, pieces),
-        in_specs=[ANY],
+        in_specs=[ANY, VMEM, VMEM],
         out_specs=[VMEM] * (2 + len(pieces)),
-        out_shape=[f32(*HALF), f32(*HALF)] + [f32(piece[2], 64, 128) for piece in pieces],
+        out_shape=[f32(*HALF), f32(*HALF)] + [f32(*rows_of(piece)) for piece in pieces],
         scratch_shapes=[
             pltpu.VMEM((2, *HALF), jnp.float32),
             pltpu.VMEM(x.shape, jnp.float32),
             pltpu.SemaphoreType.DMA((x.shape[0],)),
-            pltpu.SemaphoreType.DMA((len(pieces),)),
+            pltpu.SemaphoreType.DMA((sum(copies_of(piece) for piece in pieces),)),
         ],
         compiler_params=pltpu.CompilerParams(vmem_limit_bytes=WIDE),
         name="local_maxima",
-    )(x)
-
-
-def chip_kernel(keep_ref, got_ref, weight_ref, gain_ref, out_ref):
+    )(x, weight, gain)
+
+
+def chip_kernel(keep_ref, got_ref, out_ref):
     both = jnp.maximum(keep_ref[...], got_ref[...])
-    router = weight_ref[...] * gain_ref[...]
     for q in range(8):
-        out_ref[q, 0:8] = both
-        out_ref[q, 8] = router[0:8]
-        out_ref[q, 9] = router[8:16]
-
-
-def chip_maxima(keep, got, weight, gain):
+        out_ref[q] = both
+
+
+def chip_maxima(keep, got):
     return pl.pallas_call(
         chip_kernel,
-        in_specs=[VMEM] * 4,
-        out_specs=VMEM,
-        out_shape=f32(8, 10, 8, 128),
+        in_specs=[VMEM] * 2,
+        out_specs=VMEM,
+        out_shape=f32(8, *HALF),
         compiler_params=pltpu.CompilerParams(vmem_limit_bytes=LIMIT),
         name="chip",
-    )(keep, got, weight, gain)
-
-
-def joint_kernel(shared_ref, mine_ref, router_ref):
-    top = shared_ref[0, 0:8]
+    )(keep, got)
+
+
+def joint_kernel(shared_ref, mine_ref):
+    top = shared_ref[0]
     for q in range(1, 8):
-        top = jnp.maximum(top, shared_ref[q, 0:8])
+        top = jnp.maximum(top, shared_ref[q])
     mine_ref[...] = top
-    for q in range(8):
-        router_ref[q] = jnp.concatenate([shared_ref[q, 8], shared_ref[q, 9]], axis=0).astype(jnp.bfloat16)
 
 
 def joined(shared):
     return pl.pallas_call(
         joint_kernel,
         in_specs=[VMEM],
-        out_specs=[VMEM] * 2,
-        out_shape=[f32(*HALF), bf16(8, 16, 128)],
+        out_specs=VMEM,
+        out_shape=f32(*HALF),
         compiler_params=pltpu.CompilerParams(vmem_limit_bytes=LIMIT),
         name="joint",
     )(shared)
+
+
+def lines_kernel(pieces, weight_ref, gain_ref, *refs):
+    z, out_ref = lax.axis_index("zero_0"), refs[-1]
+    out_ref[z] = (weight_ref[...] * gain_ref[...]).astype(jnp.bfloat16)
+    for piece, ref in zip(pieces, refs):
+        out_ref[sender(piece[0])[0]] = ref[tail_of(piece), :].astype(jnp.bfloat16)
+
+
+def lines_of(pieces, blocks, weight, gain):
+    return pl.pallas_call(
+        functools.partial(lines_kernel, pieces),
+        in_specs=[VMEM] * (2 + len(pieces)),
+        out_specs=VMEM,
+        out_shape=bf16(8, 16, 128),
+        compiler_params=pltpu.CompilerParams(vmem_limit_bytes=LIMIT),
+        name="lines",
+    )(weight, gain, *blocks)
 
 
 def route_kernel(mine_ref, their_ref, out_ref):
@@ -226,32 +282,47 @@
     return [jnp.where(low, own, other), jnp.where(low, other, own)]
 
 
-def divide_rows(rows_ref, out_ref, scales, experts, start):
+def divide_rows(rows, write, scales, experts, start):
     for e in experts:
         scale = scales[(start + e) // 8]
         for r in range(0, 8, 2):
             lane = (start + e) % 8 * 8 + r
             both = jnp.concatenate([scale[:, lane : lane + 1], scale[:, lane + 1 : lane + 2]], axis=0)
-            out_ref[e, r * 8 : r * 8 + 16, :] = (rows_ref[e, r * 8 : r * 8 + 16, :] / both).astype(jnp.bfloat16)
-
-
-def ready_kernel(offset, rows_ref, mine_ref, out_ref):
-    divide_rows(rows_ref, out_ref, scales_at([mine_ref], offset), range(8), 0)
+            write(e, r, (rows(e, r) / both).astype(jnp.bfloat16))
+
+
+def reads(piece, ref):
+    return lambda e, r: expert_rows(ref, piece, e, r * 8, 16)[...]
+
+
+def writes(piece, ref):
+    def write(e, r, value):
+        expert_rows(ref, piece, e, r * 8, 16)[...] = value
+
+    return write
+
+
+def ready_kernel(piece, rows_ref, mine_ref, out_ref):
+    scales = scales_at([mine_ref], piece[0])
+    divide_rows(reads(piece, rows_ref), writes(piece, out_ref), scales, range(8), 0)
+    if piece in CARRY:
+        out_ref[tail_of(piece), :] = rows_ref[tail_of(piece), :].astype(jnp.bfloat16)
 
 
 def ready(piece, rows, mine):
     return pl.pallas_call(
-        functools.partial(ready_kernel, piece[0]),
+        functools.partial(ready_kernel, piece),
         in_specs=[VMEM, VMEM],
         out_specs=VMEM,
-        out_shape=bf16(8, 64, 128),
+        out_shape=bf16(*rows_of(piece)),
         compiler_params=pltpu.CompilerParams(vmem_limit_bytes=LIMIT),
         cost_estimate=cost(8 * 64 * 128, 6),
         name="ready",
     )(rows, mine)
 
 
-def divide_kernel(piece, x_ref, mine_ref, their_ref, out_ref, rows_ref, sems):
+def divide_kernel(piece, x_ref, mine_ref, their_ref, *refs):
+    out_ref, rows_ref, sems = refs[-3:]
     offset, start, count = piece
     z, c = there(offset)
     first = pl.multiple_of((z * 2 + c) * 64, 64)
@@ -271,31 +342,35 @@
         scales, start = scales_at([their_ref], offset), 0
     else:
         scales = scales_in_order([mine_ref, their_ref], offset)
+    if piece in CARRY:
+        out_ref[tail_of(piece), :] = (refs[0][...] * refs[1][...]).astype(jnp.bfloat16)
     for copy, part in zip(copies, parts):
         copy.wait()
-        divide_rows(rows_ref, out_ref, scales, part, start)
-
-
-def divided(piece, x, mine, theirs):
+        divide_rows(lambda e, r: rows_ref[e, r * 8 : r * 8 + 16, :], writes(piece, out_ref), scales, part, start)
+
+
+def divided(piece, x, mine, theirs, weight, gain):
     count = piece[2]
+    more = [weight, gain] if piece in CARRY else []
     return pl.pallas_call(
         functools.partial(divide_kernel, piece),
-        in_specs=[ANY, VMEM, VMEM],
-        out_specs=VMEM,
-        out_shape=bf16(count, 64, 128),
+        in_specs=[ANY] + [VMEM] * (2 + len(more)),
+        out_specs=VMEM,
+        out_shape=bf16(*rows_of(piece)),
         scratch_shapes=[pltpu.VMEM((count, 64, 128), jnp.float32), pltpu.SemaphoreType.DMA((pl.cdiv(count, 4),))],
         compiler_params=pltpu.CompilerParams(vmem_limit_bytes=WIDE),
         cost_estimate=cost(count * 64 * 128, 6),
         name="divide",
-    )(x, mine, theirs)
+    )(x, mine, theirs, *more)
 
 
 def finish_kernel(pieces, *refs):
     n = len(pieces)
     rows, (mine_ref, their_ref), outs, (scale_ref, turned_ref) = refs[:n], refs[n : n + 2], refs[n + 2 : -2], refs[-2:]
     scales = scales_in_order([mine_ref, their_ref], (0, 0))
-    for i, (_, start, count) in enumerate(pieces):
-        divide_rows(rows[i], outs[i], scales, range(count), start)
+    for i, piece in enumerate(pieces):
+        plain = writes(((0, 0), 0, 0), outs[i])
+        divide_rows(reads(piece, rows[i]), plain, scales, range(piece[2]), piece[1])
     tile = jnp.concatenate(scales, axis=1)
     turned_ref[...] = jnp.concatenate([tile, jnp.zeros((120, 128), jnp.float32)], axis=0).T
     lane = lax.broadcasted_iota(jnp.int32, (16, 128), 1)
@@ -328,10 +403,15 @@
     for i, (offset, start, count) in enumerate(pieces):
         z, c = sender(offset)
         column = pl.multiple_of((z * 2 + c) * 128, 128)
-        target = out_ref.at[pl.ds(expert_of(start, c), count), :, pl.ds(column, 128)]
-        copies.append(pltpu.make_async_copy(blocks[i], target, sems.at[i]))
+        expert, columns = expert_of(start, c), pl.ds(column, 128)
+        if len(blocks[i].shape) == 3:
+            moves = [(blocks[i], out_ref.at[pl.ds(expert, count), :, columns])]
+        else:
+            moves = [(blocks[i].at[pl.ds(e * 64, 64)], out_ref.at[expert + e, :, columns]) for e in range(count)]
+        for source, target in moves:
+            copies.append(pltpu.make_async_copy(source, target, sems.at[len(copies)]))
     if routed:
-        copies.append(pltpu.make_async_copy(refs[0], refs[2], sems.at[n]))
+        copies.append(pltpu.make_async_copy(refs[0], refs[2], sems.at[len(copies)]))
     for copy in copies:
         copy.start()
     for copy in copies:
@@ -345,7 +425,7 @@
         in_specs=[VMEM] * n + [ANY] * held + [VMEM] * routed,
         out_specs=[ANY] * (1 + routed),
         out_shape=[bf16(*shape)] + ([bf16(*router.shape)] if routed else []),
-        scratch_shapes=[pltpu.SemaphoreType.DMA((n + routed,))],
+        scratch_shapes=[pltpu.SemaphoreType.DMA((sum(b.shape[0] // 64 if b.ndim == 2 else 1 for b in blocks) + routed,))],
         input_output_aliases={n: 0} if held else {},
         compiler_params=pltpu.CompilerParams(vmem_limit_bytes=LIMIT),
         cost_estimate=cost(sum(piece[2] for piece in pieces) * 64 * 128, 4),
@@ -364,36 +444,38 @@
 
 def per_device(train_down, router_weight, router_gain):
     experts = train_down.shape[0]
-    rows = picked(RAW[:EARLY], train_down)
-    keep, give, *more = local_maxima(train_down, RAW[EARLY:])
+    router = (router_weight.T, router_gain[None, :])
+    rows = picked(RAW[:EARLY], train_down, *router)
+    keep, give, *more = local_maxima(train_down, RAW[EARLY:], *router)
     raw = []
     for i, part in enumerate([*rows, *more]):
         raw.append(sent(part, RAW[i][0]))
     given = swapped(give)
-    payload = chip_maxima(keep, given, router_weight.T, router_gain[None, :])
+    payload = chip_maxima(keep, given)
     shared = lax.all_to_all(payload, "zero_0", 0, 0, tiled=True)
-    waiting = picked(PIECES[:READY], train_down)
-    mine, lines = joined(shared)
+    waiting = picked(PIECES[:READY], train_down, *router)
+    mine = joined(shared)
     theirs = swapped(mine)
 
     kept = ((0, 0), 0, experts)
     blocks = []
     for i, piece in enumerate(PIECES):
-        part = ready(piece, waiting[i], mine) if i < READY else divided(piece, train_down, mine, theirs)
+        part = ready(piece, waiting[i], mine) if i < READY else divided(piece, train_down, mine, theirs, *router)
         blocks.append(sent(part, piece[0]))
 
+    every = dict(zip(RAW + PIECES, [*raw, *blocks]))
+    lines = lines_of(CARRY, [every[piece] for piece in CARRY], *router)
     lines = routed(lines, swapped(lines))
-    lines, _ = lax.optimization_barrier((lines, blocks[2]))
-    router = lax.all_gather(lines, "bank", axis=0, tiled=True)
-
-    early = [divided(kept, train_down, mine, theirs)]
+    gathered = lax.all_gather(lines, "bank", axis=0, tiled=True)
+
+    early = [divided(kept, train_down, mine, theirs, *router)]
     *more, scale_down = finished(RAW, raw, mine, theirs)
     pieces, blocks = (kept,) + RAW + PIECES, [*early, *more, *blocks]
     shape = (experts, 64, 2048)
     ready_down, first = None, 0
     for i, n in enumerate(GROUPS):
         group = slice(first, first + n)
-        out = placed(pieces[group], blocks[group], shape, ready_down, router if i == 1 else None)
+        out = placed(pieces[group], blocks[group], shape, ready_down, gathered if i == 1 else None)
         ready_down, first = out[0], first + n
         if i == 1:
             serve_router = out[1].T

time: 134 us -> 145 us (1.082)
  the two profiles are of different devices: /device:TPU:1 before, /device:TPU:2 now
where the time goes in v3:
time: 145 us; the launch traced here: 144 us
  starting transfers between devices  57.1 us (39%)
  Pallas kernels  36.4 us (25%)
  waiting for transfers between devices  35.3 us (24%)
  blocking collectives  12.5 us (9%)
    ppermute x22, starting transfers between devices, sent(): return lax.ppermute(piece, ZERO, pairs)  48.6 us
    ppermute x22, waiting for transfers between devices, sent(): return lax.ppermute(piece, ZERO, pairs)  29.5 us
    pallas_call x16, Pallas kernels, divided(): pl.pallas_call(functools.partial(divide_kernel, piece), in_specs=[ANY] +...  22.9 us
    all_gather x1, blocking collectives, per_device(): gathered = lax.all_gather(lines, 'bank', axis=0, tiled=True)  12.5 us
    all_to_all x1, starting transfers between devices, per_device(): shared = lax.all_to_all(payload, 'zero_0', 0, 0, tiled=True)  8.47 us
    all_to_all x1, waiting for transfers between devices, per_device(): shared = lax.all_to_all(payload, 'zero_0', 0, 0, tiled=True)  5.82 us
    pallas_call x4, Pallas kernels, placed(): pl.pallas_call(functools.partial(place_kernel, tuple(pieces), held, route...  4.72 us
    pallas_call x1, Pallas kernels, local_maxima(): pl.pallas_call(functools.partial(maxima_kernel, pieces), in_specs=[ANY, V...  4.29 us
  transfers between devices with their start and end apart: 23, of which 4 were waited for; matrix products, arithmetic and copies ran while one was open for 0% of the time, Pallas kernels for 21%

profile of v3, /device:TPU:2, one launch (start us, length us, event | category | flops | bytes accessed | tf_op | source)
XLA Modules:
  0.0 143.9 jit_solution(10051051745239463747)
XLA Ops:
  2.0 4.3 %local_maxima.1 = (f32[8,8,128]{2,1,0:T(8,128)S(1)}, f32[8,8,128]{2,1,0:T(8,128)S(1)}, f32[528,128]{1,0:T(8,128)S(1)}) custom-call(f32[16,1024,128]{2,1,0:T(8,128)} %x_ref.37, f32[16,128]{1,0:T(8,128)S(1)} %bitcast.3, f32[1,128]{1,0:T(1,128)S(1)} %bitcast.10), custom_call_target="tpu_custom_call" | custom-call | tf_op jit(solution)/shard_map/local_maxima/pallas_call | solution.py:185
  8.3 8.5 %all-to-all-start = ((f32[8,8,8,128]{3,2,1,0:T(8,128)}), f32[8,8,8,128]{3,2,1,0:T(8,128)S(1)}, u32[]{:S(2)}, u32[]{:S(2)}) async-start(f32[8,8,8,128]{3,2,1,0:T(8,128)} %chip.1), calls=%async_computation | async-start | bytes 524288 | tf_op jit(solution)/shard_map/all_to_all | solution.py:455
  17.8 6.0 %collective-permute-start.13 = (f32[8,64,128]{2,1,0:T(8,128)S(1)}, f32[8,64,128]{2,1,0:T(8,128)S(1)}, u32[]{:S(2)}, u32[]{:S(2)}) collective-permute-start(f32[8,64,128]{2,1,0:T(8,128)S(1)} %pick.2), channel_id=1, source_target_pairs={{0,8},{1,9},{2,10},{3,11},{4,12},{5,13},{6,14},{7,15},{8,0},{9,1},... | collective-permute-start | bytes 786440 | tf_op jit(solution)/shard_map/ppermute | solution.py:438
  24.4 5.8 %all-to-all-done.shared_ref = f32[8,8,8,128]{3,2,1,0:T(8,128)S(1)} async-done(((f32[8,8,8,128]{3,2,1,0:T(8,128)}), f32[8,8,8,128]{3,2,1,0:T(8,128)S(1)}, u32[]{:S(2)}, u32[]{:S(2)}) %all-to-all-start) | async-done | bytes 262176 | tf_op jit(solution)/shard_map/all_to_all | solution.py:455
  31.8 11.8 %collective-permute-start.15 = (bf16[528,128]{1,0:T(8,128)(2,1)S(1)}, bf16[528,128]{1,0:T(8,128)(2,1)S(1)}, u32[]{:S(2)}, u32[]{:S(2)}) collective-permute-start(bf16[528,128]{1,0:T(8,128)(2,1)S(1)} %ready.2), channel_id=1, source_target_pairs={{0,6},{1,11},{2,8},{3,13},{4,10},{5,15},{6,12},{7,1},{8,14},{9,3},... | collective-permute-start | bytes 405512 | tf_op jit(solution)/shard_map/ppermute | solution.py:438
  43.9 1.5 %divide.29 = bf16[16,64,128]{2,1,0:T(8,128)(2,1)S(1)} custom-call(f32[16,1024,128]{2,1,0:T(8,128)} %x_ref.37, f32[8,8,128]{2,1,0:T(8,128)S(1)} %joint.1.mine_ref.refs_2_, f32[8,8,128]{2,1,0:T(8,128)S(1)} %collective-permute-done.1.their_ref.refs_3_), custom_call_target="tpu_custom_call" | custom-call | flops 1048576 | bytes 786432 | tf_op jit(solution)/shard_map/divide/pallas_call | solution.py:355
  45.4 4.6 %collective-permute-start.18 = (bf16[16,64,128]{2,1,0:T(8,128)(2,1)S(1)}, bf16[16,64,128]{2,1,0:T(8,128)(2,1)S(1)}, u32[]{:S(2)}, u32[]{:S(2)}) collective-permute-start(bf16[16,64,128]{2,1,0:T(8,128)(2,1)S(1)} %divide.29), channel_id=1, source_target_pairs={{0,7},{1,10},{2,9},{3,12},{4,11},{5,14},{6,13},{7,0},{8,15},{9,2},... | collective-permute-start | bytes 786440 | tf_op jit(solution)/shard_map/ppermute | solution.py:438
  50.0 1.5 %divide.30 = bf16[16,64,128]{2,1,0:T(8,128)(2,1)S(1)} custom-call(f32[16,1024,128]{2,1,0:T(8,128)} %x_ref.37, f32[8,8,128]{2,1,0:T(8,128)S(1)} %joint.1.mine_ref.refs_2_, f32[8,8,128]{2,1,0:T(8,128)S(1)} %collective-permute-done.1.their_ref.refs_3_), custom_call_target="tpu_custom_call" | custom-call | flops 1048576 | bytes 786432 | tf_op jit(solution)/shard_map/divide/pallas_call | solution.py:355
  51.6 1.2 divide.28
  52.9 3.9 %collective-permute-start.17 = (bf16[528,128]{1,0:T(8,128)(2,1)S(1)}, bf16[528,128]{1,0:T(8,128)(2,1)S(1)}, u32[]{:S(2)}, u32[]{:S(2)}) collective-permute-start(bf16[528,128]{1,0:T(8,128)(2,1)S(1)} %divide.28), channel_id=1, source_target_pairs={{0,8},{1,9},{2,10},{3,11},{4,12},{5,13},{6,14},{7,15},{8,0},{9,1},... | collective-permute-start | bytes 405512 | tf_op jit(solution)/shard_map/ppermute | solution.py:438
  56.8 1.2 divide.24
  58.0 4.3 %collective-permute-start.10 = (bf16[8,64,128]{2,1,0:T(8,128)(2,1)S(1)}, bf16[8,64,128]{2,1,0:T(8,128)(2,1)S(1)}, u32[]{:S(2)}, u32[]{:S(2)}) collective-permute-start(bf16[8,64,128]{2,1,0:T(8,128)(2,1)S(1)} %divide.24), channel_id=1, source_target_pairs={{0,6},{1,11},{2,8},{3,13},{4,10},{5,15},{6,12},{7,1},{8,14},{9,3},... | collective-permute-start | bytes 393224 | tf_op jit(solution)/shard_map/ppermute | solution.py:438
  64.4 1.5 %divide.31 = bf16[1040,128]{1,0:T(8,128)(2,1)S(1)} custom-call(f32[16,1024,128]{2,1,0:T(8,128)} %x_ref.37, f32[8,8,128]{2,1,0:T(8,128)S(1)} %joint.1.mine_ref.refs_2_, f32[8,8,128]{2,1,0:T(8,128)S(1)} %collective-permute-done.1.their_ref.refs_3_, f32[16,128]{1,0:T(8,128)S(1)} %bitcast.6, f32[1,128]{1,0:T(1,128)S(1)} %bitcast.13), custom_call_target="tpu_custom_call" | custom-call | flops 1048576 | bytes 786432 | tf_op jit(solution)/shard_map/divide/pallas_call | solution.py:355
  65.9 22.7 %collective-permute-done.10.refs_3_ = bf16[8,64,128]{2,1,0:T(8,128)(2,1)S(1)} collective-permute-done((bf16[8,64,128]{2,1,0:T(8,128)(2,1)S(1)}, bf16[8,64,128]{2,1,0:T(8,128)(2,1)S(1)}, u32[]{:S(2)}, u32[]{:S(2)}) %collective-permute-start.10) | collective-permute-done | bytes 131104 | tf_op jit(solution)/shard_map/ppermute | solution.py:438
  88.6 1.5 %divide.21 = bf16[1040,128]{1,0:T(8,128)(2,1)S(1)} custom-call(f32[16,1024,128]{2,1,0:T(8,128)} %x_ref.37, f32[8,8,128]{2,1,0:T(8,128)S(1)} %joint.1.mine_ref.refs_2_, f32[8,8,128]{2,1,0:T(8,128)S(1)} %collective-permute-done.1.their_ref.refs_3_, f32[16,128]{1,0:T(8,128)S(1)} %bitcast.7, f32[1,128]{1,0:T(1,128)S(1)} %bitcast.14), custom_call_target="tpu_custom_call" | custom-call | flops 1048576 | bytes 786432 | tf_op jit(solution)/shard_map/divide/pallas_call | solution.py:355
  90.1 1.5 %divide.22 = bf16[1040,128]{1,0:T(8,128)(2,1)S(1)} custom-call(f32[16,1024,128]{2,1,0:T(8,128)} %x_ref.37, f32[8,8,128]{2,1,0:T(8,128)S(1)} %joint.1.mine_ref.refs_2_, f32[8,8,128]{2,1,0:T(8,128)S(1)} %collective-permute-done.1.their_ref.refs_3_, f32[16,128]{1,0:T(8,128)S(1)} %bitcast.8, f32[1,128]{1,0:T(1,128)S(1)} %bitcast.15), custom_call_target="tpu_custom_call" | custom-call | flops 1048576 | bytes 786432 | tf_op jit(solution)/shard_map/divide/pallas_call | solution.py:355
  91.6 3.5 %collective-permute-start.7 = (bf16[1040,128]{1,0:T(8,128)(2,1)S(1)}, bf16[1040,128]{1,0:T(8,128)(2,1)S(1)}, u32[]{:S(2)}, u32[]{:S(2)}) collective-permute-start(bf16[1040,128]{1,0:T(8,128)(2,1)S(1)} %divide.21), channel_id=1, source_target_pairs={{0,14},{1,3},{2,0},{3,5},{4,2},{5,7},{6,4},{7,9},{8,6},{9,11},{10,... | collective-permute-start | bytes 798728 | tf_op jit(solution)/shard_map/ppermute | solution.py:438
  95.1 1.5 %divide.26 = bf16[16,64,128]{2,1,0:T(8,128)(2,1)S(1)} custom-call(f32[16,1024,128]{2,1,0:T(8,128)} %x_ref.37, f32[8,8,128]{2,1,0:T(8,128)S(1)} %joint.1.mine_ref.refs_2_, f32[8,8,128]{2,1,0:T(8,128)S(1)} %collective-permute-done.1.their_ref.refs_3_), custom_call_target="tpu_custom_call" | custom-call | flops 1048576 | bytes 786432 | tf_op jit(solution)/shard_map/divide/pallas_call | solution.py:355
  96.7 1.5 %divide.23 = bf16[16,64,128]{2,1,0:T(8,128)(2,1)S(1)} custom-call(f32[16,1024,128]{2,1,0:T(8,128)} %x_ref.37, f32[8,8,128]{2,1,0:T(8,128)S(1)} %joint.1.mine_ref.refs_2_, f32[8,8,128]{2,1,0:T(8,128)S(1)} %collective-permute-done.1.their_ref.refs_3_), custom_call_target="tpu_custom_call" | custom-call | flops 1048576 | bytes 786432 | tf_op jit(solution)/shard_map/divide/pallas_call | solution.py:355
  98.2 3.6 %collective-permute-start.9 = (bf16[16,64,128]{2,1,0:T(8,128)(2,1)S(1)}, bf16[16,64,128]{2,1,0:T(8,128)(2,1)S(1)}, u32[]{:S(2)}, u32[]{:S(2)}) collective-permute-start(bf16[16,64,128]{2,1,0:T(8,128)(2,1)S(1)} %divide.23), channel_id=1, source_target_pairs={{0,9},{1,8},{2,11},{3,10},{4,13},{5,12},{6,15},{7,14},{8,1},{9,0},... | collective-permute-start | bytes 786440 | tf_op jit(solution)/shard_map/ppermute | solution.py:438
  101.8 1.5 %divide.19 = bf16[16,64,128]{2,1,0:T(8,128)(2,1)S(1)} custom-call(f32[16,1024,128]{2,1,0:T(8,128)} %x_ref.37, f32[8,8,128]{2,1,0:T(8,128)S(1)} %joint.1.mine_ref.refs_2_, f32[8,8,128]{2,1,0:T(8,128)S(1)} %collective-permute-done.1.their_ref.refs_3_), custom_call_target="tpu_custom_call" | custom-call | flops 1048576 | bytes 786432 | tf_op jit(solution)/shard_map/divide/pallas_call | solution.py:355
  103.3 1.5 %divide.20 = bf16[16,64,128]{2,1,0:T(8,128)(2,1)S(1)} custom-call(f32[16,1024,128]{2,1,0:T(8,128)} %x_ref.37, f32[8,8,128]{2,1,0:T(8,128)S(1)} %joint.1.mine_ref.refs_2_, f32[8,8,128]{2,1,0:T(8,128)S(1)} %collective-permute-done.1.their_ref.refs_3_), custom_call_target="tpu_custom_call" | custom-call | flops 1048576 | bytes 786432 | tf_op jit(solution)/shard_map/divide/pallas_call | solution.py:355
  104.9 1.3 collective-permute-start.5
  106.1 2.2 %collective-permute-start.6 = (bf16[16,64,128]{2,1,0:T(8,128)(2,1)S(1)}, bf16[16,64,128]{2,1,0:T(8,128)(2,1)S(1)}, u32[]{:S(2)}, u32[]{:S(2)}) collective-permute-start(bf16[16,64,128]{2,1,0:T(8,128)(2,1)S(1)} %divide.20), channel_id=1, source_target_pairs={{0,15},{1,2},{2,1},{3,4},{4,3},{5,6},{6,5},{7,8},{8,7},{9,10},{10,... | collective-permute-start | bytes 786440 | tf_op jit(solution)/shard_map/ppermute | solution.py:438
  108.3 1.5 %divide.17 = bf16[16,64,128]{2,1,0:T(8,128)(2,1)S(1)} custom-call(f32[16,1024,128]{2,1,0:T(8,128)} %x_ref.37, f32[8,8,128]{2,1,0:T(8,128)S(1)} %joint.1.mine_ref.refs_2_, f32[8,8,128]{2,1,0:T(8,128)S(1)} %collective-permute-done.1.their_ref.refs_3_), custom_call_target="tpu_custom_call" | custom-call | flops 1048576 | bytes 786432 | tf_op jit(solution)/shard_map/divide/pallas_call | solution.py:355
  109.8 1.5 %divide.16 = bf16[16,64,128]{2,1,0:T(8,128)(2,1)S(1)} custom-call(f32[16,1024,128]{2,1,0:T(8,128)} %x_ref.37, f32[8,8,128]{2,1,0:T(8,128)S(1)} %joint.1.mine_ref.refs_2_, f32[8,8,128]{2,1,0:T(8,128)S(1)} %collective-permute-done.1.their_ref.refs_3_), custom_call_target="tpu_custom_call" | custom-call | flops 1048576 | bytes 786432 | tf_op jit(solution)/shard_map/divide/pallas_call | solution.py:355
  112.1 5.6 %collective-permute-done.8.refs_5_.refs_1_ = bf16[1040,128]{1,0:T(8,128)(2,1)S(1)} collective-permute-done((bf16[1040,128]{1,0:T(8,128)(2,1)S(1)}, bf16[1040,128]{1,0:T(8,128)(2,1)S(1)}, u32[]{:S(2)}, u32[]{:S(2)}) %collective-permute-start.8) | collective-permute-done | bytes 266272 | tf_op jit(solution)/shard_map/ppermute | solution.py:438
  117.8 4.8 %collective-permute-start.21 = (bf16[8,16,128]{2,1,0:T(8,128)(2,1)S(1)}, bf16[8,16,128]{2,1,0:T(8,128)(2,1)S(1)}, u32[]{:S(2)}, u32[]{:S(2)}) collective-permute-start(bf16[8,16,128]{2,1,0:T(8,128)(2,1)S(1)} %lines.1.mine_ref), channel_id=1, source_target_pairs={{0,1},{1,0},{2,3},{3,2},{4,5},{5,4},{6,7},{7,6},{8,9},{9,8},{10,11... | collective-permute-start | bytes 98312 | tf_op jit(solution)/shard_map/ppermute | solution.py:438
  123.9 1.5 %divide.27.refs_0_ = bf16[16,64,128]{2,1,0:T(8,128)(2,1)S(1)} custom-call(f32[16,1024,128]{2,1,0:T(8,128)} %x_ref.37, f32[8,8,128]{2,1,0:T(8,128)S(1)} %joint.1.mine_ref.refs_2_, f32[8,8,128]{2,1,0:T(8,128)S(1)} %collective-permute-done.1.their_ref.refs_3_), custom_call_target="tpu_custom_call" | custom-call | flops 1048576 | bytes 786432 | tf_op jit(solution)/shard_map/divide/pallas_call | solution.py:355
  126.4 1.6 %place.4.refs_6_ = bf16[16,64,2048]{2,1,0:T(8,128)(2,1)} custom-call(bf16[16,64,128]{2,1,0:T(8,128)(2,1)S(1)} %divide.27.refs_0_, bf16[8,64,128]{2,1,0:T(8,128)(2,1)S(1)} %get-tuple-element.16.refs_1_, bf16[8,64,128]{2,1,0:T(8,128)(2,1)S(1)} %get-tuple-element.17.refs_2_, bf16[528,128]{1,0:T(8,128)(2,1)S(1)} %collective-permute-done.15.refs_3_.refs_2_, ...), custom_call_target="tpu_custom_call" | custom-call | flops 6815744 | bytes 3407872 | tf_op jit(solution)/shard_map/place/pallas_call | solution.py:423
  128.0 12.5 %all_gather.3.refs_7_ = bf16[64,2048]{1,0:T(8,128)(2,1)S(1)} all-gather(bf16[16,2048]{1,0:T(8,128)(2,1)S(1)} %route.1), channel_id=1, replica_groups=mesh['unit'=4,'bank'=4,'zero_0'=8,'zero_1'=2] {'bank'}, dimensions={0}, use_global_device_ids=true | all-gather | bytes 327680 | tf_op jit(solution)/shard_map/all_gather | solution.py:469
  140.5 1.5 %place.5 = (bf16[16,64,2048]{2,1,0:T(8,128)(2,1)}, bf16[64,2048]{1,0:T(8,128)(2,1)}) custom-call(bf16[1040,128]{1,0:T(8,128)(2,1)S(1)} %collective-permute-done.7.refs_6_.refs_0_, bf16[1040,128]{1,0:T(8,128)(2,1)S(1)} %collective-permute-done.8.refs_5_.refs_1_, ...), custom_call_target="tpu_custom_call", output_to_operand_aliasing={{0}: (6, {})} | custom-call | flops 5242880 | bytes 2621440 | tf_op jit(solution)/shard_map/place/pallas_call | solution.py:423
  (53 shorter events, 14.1 us)
Async XLA Ops:
  0.6 0.7 copy-start
  1.3 0.7 copy-start.2
  6.3 1.3 collective-permute-start
  8.3 21.9 %all-to-all-start = ((f32[8,8,8,128]{3,2,1,0:T(8,128)}), f32[8,8,8,128]{3,2,1,0:T(8,128)S(1)}, u32[]{:S(2)}, u32[]{:S(2)}) async-start(f32[8,8,8,128]{3,2,1,0:T(8,128)} %chip.1), calls=%async_computation | async-start | bytes 524288 | tf_op jit(solution)/shard_map/all_to_all | solution.py:455
  16.8 13.5 %copy-start.1 = (f32[128,16]{0,1:T(8,128)S(1)}, f32[128,16]{0,1:T(8,128)}, u32[]{:S(2)}) copy-start(f32[128,16]{0,1:T(8,128)} %param.4) | copy-start | bytes 24580
  16.8 13.5 %copy-start.3 = (f32[128]{0:T(128)S(1)}, f32[128]{0:T(128)}, u32[]{:S(2)}) copy-start(f32[128]{0:T(128)} %param.5) | copy-start | bytes 1540
  17.8 33.8 %collective-permute-start.13 = (f32[8,64,128]{2,1,0:T(8,128)S(1)}, f32[8,64,128]{2,1,0:T(8,128)S(1)}, u32[]{:S(2)}, u32[]{:S(2)}) collective-permute-start(f32[8,64,128]{2,1,0:T(8,128)S(1)} %pick.2), channel_id=1, source_target_pairs={{0,8},{1,9},{2,10},{3,11},{4,12},{5,13},{6,14},{7,15},{8,0},{9,1},... | collective-permute-start | bytes 786440 | tf_op jit(solution)/shard_map/ppermute | solution.py:438
  23.8 29.1 %collective-permute-start.14 = (f32[528,128]{1,0:T(8,128)S(1)}, f32[528,128]{1,0:T(8,128)S(1)}, u32[]{:S(2)}, u32[]{:S(2)}) collective-permute-start(f32[528,128]{1,0:T(8,128)S(1)} %get-tuple-element.15), channel_id=1, source_target_pairs={{0,4},{1,13},{2,6},{3,15},{4,8},{5,1},{6,10},{7,3},{8,12},{9,5},{1... | collective-permute-start | bytes 811016 | tf_op jit(solution)/shard_map/ppermute | solution.py:438
  30.2 13.7 %collective-permute-start.1 = (f32[8,8,128]{2,1,0:T(8,128)S(1)}, f32[8,8,128]{2,1,0:T(8,128)S(1)}, u32[]{:S(2)}, u32[]{:S(2)}) collective-permute-start(f32[8,8,128]{2,1,0:T(8,128)S(1)} %joint.1.mine_ref.refs_2_), channel_id=1, source_target_pairs={{0,1},{1,0},{2,3},{3,2},{4,5},{5,4},{6,7},{7,6},{8,9},{9,8},{10,11... | collective-permute-start | bytes 98312 | tf_op jit(solution)/shard_map/ppermute | solution.py:438
  31.8 26.2 %collective-permute-start.15 = (bf16[528,128]{1,0:T(8,128)(2,1)S(1)}, bf16[528,128]{1,0:T(8,128)(2,1)S(1)}, u32[]{:S(2)}, u32[]{:S(2)}) collective-permute-start(bf16[528,128]{1,0:T(8,128)(2,1)S(1)} %ready.2), channel_id=1, source_target_pairs={{0,6},{1,11},{2,8},{3,13},{4,10},{5,15},{6,12},{7,1},{8,14},{9,3},... | collective-permute-start | bytes 405512 | tf_op jit(solution)/shard_map/ppermute | solution.py:438
  43.8 19.7 %collective-permute-start.16 = (bf16[528,128]{1,0:T(8,128)(2,1)S(1)}, bf16[528,128]{1,0:T(8,128)(2,1)S(1)}, u32[]{:S(2)}, u32[]{:S(2)}) collective-permute-start(bf16[528,128]{1,0:T(8,128)(2,1)S(1)} %ready.3), channel_id=1, source_target_pairs={{0,10},{1,7},{2,12},{3,9},{4,14},{5,11},{6,0},{7,13},{8,2},{9,15},... | collective-permute-start | bytes 405512 | tf_op jit(solution)/shard_map/ppermute | solution.py:438
  45.4 51.2 %collective-permute-start.18 = (bf16[16,64,128]{2,1,0:T(8,128)(2,1)S(1)}, bf16[16,64,128]{2,1,0:T(8,128)(2,1)S(1)}, u32[]{:S(2)}, u32[]{:S(2)}) collective-permute-start(bf16[16,64,128]{2,1,0:T(8,128)(2,1)S(1)} %divide.29), channel_id=1, source_target_pairs={{0,7},{1,10},{2,9},{3,12},{4,11},{5,14},{6,13},{7,0},{8,15},{9,2},... | collective-permute-start | bytes 786440 | tf_op jit(solution)/shard_map/ppermute | solution.py:438
  51.5 46.7 %collective-permute-start.19 = (bf16[16,64,128]{2,1,0:T(8,128)(2,1)S(1)}, bf16[16,64,128]{2,1,0:T(8,128)(2,1)S(1)}, u32[]{:S(2)}, u32[]{:S(2)}) collective-permute-start(bf16[16,64,128]{2,1,0:T(8,128)(2,1)S(1)} %divide.30), channel_id=1, source_target_pairs={{0,11},{1,6},{2,13},{3,8},{4,15},{5,10},{6,1},{7,12},{8,3},{9,14},... | collective-permute-start | bytes 786440 | tf_op jit(solution)/shard_map/ppermute | solution.py:438
  52.9 42.2 %collective-permute-start.17 = (bf16[528,128]{1,0:T(8,128)(2,1)S(1)}, bf16[528,128]{1,0:T(8,128)(2,1)S(1)}, u32[]{:S(2)}, u32[]{:S(2)}) collective-permute-start(bf16[528,128]{1,0:T(8,128)(2,1)S(1)} %divide.28), channel_id=1, source_target_pairs={{0,8},{1,9},{2,10},{3,11},{4,12},{5,13},{6,14},{7,15},{8,0},{9,1},... | collective-permute-start | bytes 405512 | tf_op jit(solution)/shard_map/ppermute | solution.py:438
  58.0 30.6 %collective-permute-start.10 = (bf16[8,64,128]{2,1,0:T(8,128)(2,1)S(1)}, bf16[8,64,128]{2,1,0:T(8,128)(2,1)S(1)}, u32[]{:S(2)}, u32[]{:S(2)}) collective-permute-start(bf16[8,64,128]{2,1,0:T(8,128)(2,1)S(1)} %divide.24), channel_id=1, source_target_pairs={{0,6},{1,11},{2,8},{3,13},{4,10},{5,15},{6,12},{7,1},{8,14},{9,3},... | collective-permute-start | bytes 393224 | tf_op jit(solution)/shard_map/ppermute | solution.py:438
  63.5 28.1 %collective-permute-start.11 = (bf16[8,64,128]{2,1,0:T(8,128)(2,1)S(1)}, bf16[8,64,128]{2,1,0:T(8,128)(2,1)S(1)}, u32[]{:S(2)}, u32[]{:S(2)}) collective-permute-start(bf16[8,64,128]{2,1,0:T(8,128)(2,1)S(1)} %divide.25), channel_id=1, source_target_pairs={{0,10},{1,7},{2,12},{3,9},{4,14},{5,11},{6,0},{7,13},{8,2},{9,15},... | collective-permute-start | bytes 393224 | tf_op jit(solution)/shard_map/ppermute | solution.py:438
  88.6 17.6 %collective-permute-start.20 = (bf16[1040,128]{1,0:T(8,128)(2,1)S(1)}, bf16[1040,128]{1,0:T(8,128)(2,1)S(1)}, u32[]{:S(2)}, u32[]{:S(2)}) collective-permute-start(bf16[1040,128]{1,0:T(8,128)(2,1)S(1)} %divide.31), channel_id=1, source_target_pairs={{0,2},{1,15},{2,4},{3,1},{4,6},{5,3},{6,8},{7,5},{8,10},{9,7},{10,... | collective-permute-start | bytes 798728 | tf_op jit(solution)/shard_map/ppermute | solution.py:438
  91.6 19.7 %collective-permute-start.7 = (bf16[1040,128]{1,0:T(8,128)(2,1)S(1)}, bf16[1040,128]{1,0:T(8,128)(2,1)S(1)}, u32[]{:S(2)}, u32[]{:S(2)}) collective-permute-start(bf16[1040,128]{1,0:T(8,128)(2,1)S(1)} %divide.21), channel_id=1, source_target_pairs={{0,14},{1,3},{2,0},{3,5},{4,2},{5,7},{6,4},{7,9},{8,6},{9,11},{10,... | collective-permute-start | bytes 798728 | tf_op jit(solution)/shard_map/ppermute | solution.py:438
  95.1 22.6 %collective-permute-start.8 = (bf16[1040,128]{1,0:T(8,128)(2,1)S(1)}, bf16[1040,128]{1,0:T(8,128)(2,1)S(1)}, u32[]{:S(2)}, u32[]{:S(2)}) collective-permute-start(bf16[1040,128]{1,0:T(8,128)(2,1)S(1)} %divide.22), channel_id=1, source_target_pairs={{0,12},{1,5},{2,14},{3,7},{4,0},{5,9},{6,2},{7,11},{8,4},{9,13},{1... | collective-permute-start | bytes 798728 | tf_op jit(solution)/shard_map/ppermute | solution.py:438
  96.6 8.2 %collective-permute-start.12 = (bf16[16,64,128]{2,1,0:T(8,128)(2,1)S(1)}, bf16[16,64,128]{2,1,0:T(8,128)(2,1)S(1)}, u32[]{:S(2)}, u32[]{:S(2)}) collective-permute-start(bf16[16,64,128]{2,1,0:T(8,128)(2,1)S(1)} %divide.26), channel_id=1, source_target_pairs={{0,1},{1,0},{2,3},{3,2},{4,5},{5,4},{6,7},{7,6},{8,9},{9,8},{10,11... | collective-permute-start | bytes 786440 | tf_op jit(solution)/shard_map/ppermute | solution.py:438
  98.2 19.5 %collective-permute-start.9 = (bf16[16,64,128]{2,1,0:T(8,128)(2,1)S(1)}, bf16[16,64,128]{2,1,0:T(8,128)(2,1)S(1)}, u32[]{:S(2)}, u32[]{:S(2)}) collective-permute-start(bf16[16,64,128]{2,1,0:T(8,128)(2,1)S(1)} %divide.23), channel_id=1, source_target_pairs={{0,9},{1,8},{2,11},{3,10},{4,13},{5,12},{6,15},{7,14},{8,1},{9,0},... | collective-permute-start | bytes 786440 | tf_op jit(solution)/shard_map/ppermute | solution.py:438
  104.9 37.1 %collective-permute-start.5 = (bf16[16,64,128]{2,1,0:T(8,128)(2,1)S(1)}, bf16[16,64,128]{2,1,0:T(8,128)(2,1)S(1)}, u32[]{:S(2)}, u32[]{:S(2)}) collective-permute-start(bf16[16,64,128]{2,1,0:T(8,128)(2,1)S(1)} %divide.19), channel_id=1, source_target_pairs={{0,3},{1,14},{2,5},{3,0},{4,7},{5,2},{6,9},{7,4},{8,11},{9,6},{10,... | collective-permute-start | bytes 786440 | tf_op jit(solution)/shard_map/ppermute | solution.py:438
  106.1 35.9 %collective-permute-start.6 = (bf16[16,64,128]{2,1,0:T(8,128)(2,1)S(1)}, bf16[16,64,128]{2,1,0:T(8,128)(2,1)S(1)}, u32[]{:S(2)}, u32[]{:S(2)}) collective-permute-start(bf16[16,64,128]{2,1,0:T(8,128)(2,1)S(1)} %divide.20), channel_id=1, source_target_pairs={{0,15},{1,2},{2,1},{3,4},{4,3},{5,6},{6,5},{7,8},{8,7},{9,10},{10,... | collective-permute-start | bytes 786440 | tf_op jit(solution)/shard_map/ppermute | solution.py:438
  111.3 31.6 %collective-permute-start.3 = (bf16[16,64,128]{2,1,0:T(8,128)(2,1)S(1)}, bf16[16,64,128]{2,1,0:T(8,128)(2,1)S(1)}, u32[]{:S(2)}, u32[]{:S(2)}) collective-permute-start(bf16[16,64,128]{2,1,0:T(8,128)(2,1)S(1)} %divide.17), channel_id=1, source_target_pairs={{0,13},{1,4},{2,15},{3,6},{4,1},{5,8},{6,3},{7,10},{8,5},{9,12},{1... | collective-permute-start | bytes 786440 | tf_op jit(solution)/shard_map/ppermute | solution.py:438
  117.7 25.2 %collective-permute-start.2 = (bf16[16,64,128]{2,1,0:T(8,128)(2,1)S(1)}, bf16[16,64,128]{2,1,0:T(8,128)(2,1)S(1)}, u32[]{:S(2)}, u32[]{:S(2)}) collective-permute-start(bf16[16,64,128]{2,1,0:T(8,128)(2,1)S(1)} %divide.16), channel_id=1, source_target_pairs={{0,5},{1,12},{2,7},{3,14},{4,9},{5,0},{6,11},{7,2},{8,13},{9,4},{1... | collective-permute-start | bytes 786440 | tf_op jit(solution)/shard_map/ppermute | solution.py:438
  117.8 6.0 %collective-permute-start.21 = (bf16[8,16,128]{2,1,0:T(8,128)(2,1)S(1)}, bf16[8,16,128]{2,1,0:T(8,128)(2,1)S(1)}, u32[]{:S(2)}, u32[]{:S(2)}) collective-permute-start(bf16[8,16,128]{2,1,0:T(8,128)(2,1)S(1)} %lines.1.mine_ref), channel_id=1, source_target_pairs={{0,1},{1,0},{2,3},{3,2},{4,5},{5,4},{6,7},{7,6},{8,9},{9,8},{10,11... | collective-permute-start | bytes 98312 | tf_op jit(solution)/shard_map/ppermute | solution.py:438
  123.8 18.2 %collective-permute-start.4 = (bf16[8,64,128]{2,1,0:T(8,128)(2,1)S(1)}, bf16[8,64,128]{2,1,0:T(8,128)(2,1)S(1)}, u32[]{:S(2)}, u32[]{:S(2)}) collective-permute-start(bf16[8,64,128]{2,1,0:T(8,128)(2,1)S(1)} %divide.18), channel_id=1, source_target_pairs={{0,4},{1,13},{2,6},{3,15},{4,8},{5,1},{6,10},{7,3},{8,12},{9,5},{1... | collective-permute-start | bytes 393224 | tf_op jit(solution)/shard_map/ppermute | solution.py:438
